TPU v7x, 32 devices: a whole 2x2x4 slice. The times are simulated.
32 devices in a mesh: data: 4 (over z), cp: 8 (over y, x, core).
Axes of the slice: x: 2, y: 2, z: 4, core: 2. Of those that a mesh axis runs over, the one named last changes fastest.
Arguments:
- q: bfloat16 [32768, 4, 128], P(('data', 'cp')), parts along dimension 0
- k: bfloat16 [32768, 4, 128], P(('data', 'cp')), parts along dimension 0
- v: bfloat16 [32768, 4, 128], P(('data', 'cp')), parts along dimension 0
- o: bfloat16 [32768, 4, 128], P(('data', 'cp')), parts along dimension 0
- dout: bfloat16 [32768, 4, 128], P(('data', 'cp')), parts along dimension 0
- lse: float32 [4, 32768], P(None, ('data', 'cp')), parts along dimension 1
Outputs:
- output 1: bfloat16 [32768, 4, 128], P(('data', 'cp')), parts along dimension 0
- output 2: bfloat16 [32768, 4, 128], P(('data', 'cp')), parts along dimension 0
- output 3: bfloat16 [32768, 4, 128], P(('data', 'cp')), parts along dimension 0
There are 4 independent parts. A program takes and returns all parts, laid end to end along the dimension named above; each array names one.
All inputs are finite; a program needn't handle non-finite values.
Results may differ from a plain program's by a relative error of at most 0.001.
Values are sent between devices in bfloat16 or wider.
A program may use at most 1 GiB of HBM per device.

v0:
```python
import jax
import jax.numpy as jnp
from jax import lax
from jax.sharding import PartitionSpec as P

TILE = 512


def _tiles(q, dout, o, lse, n, me):
    c, h, d = q.shape
    m = c // TILE
    dd = jnp.einsum('qhd,qhd->hq', dout, o, preferred_element_type=jnp.float32)
    qpos = jnp.arange(c, dtype=jnp.int32) * n + me
    return (q.reshape(m, TILE, h, d), dout.reshape(m, TILE, h, d),
            lse.reshape(h, m, TILE).transpose(1, 0, 2),
            dd.reshape(h, m, TILE).transpose(1, 0, 2),
            qpos.reshape(m, TILE))


def _block_grads(xs, kb, vb, kpos, gk, gv, scale):
    f32 = jnp.float32

    def body(carry, x):
        gk, gv = carry
        qt, dt, lt, et, pt = x
        s = jnp.einsum('qhd,khd->hqk', qt, kb, preferred_element_type=f32) * scale
        mask = kpos[None, :] <= pt[:, None]
        p = jnp.where(mask[None], jnp.exp(s - lt[:, :, None]), 0.0)
        gv = gv + jnp.einsum('hqk,qhd->khd', p.astype(jnp.bfloat16), dt, preferred_element_type=f32)
        dp = jnp.einsum('qhd,khd->hqk', dt, vb, preferred_element_type=f32)
        ds = (p * (dp - et[:, :, None])).astype(jnp.bfloat16)
        dq = jnp.einsum('hqk,khd->qhd', ds, kb, preferred_element_type=f32) * scale
        gk = gk + jnp.einsum('hqk,qhd->khd', ds, qt, preferred_element_type=f32) * scale
        return (gk, gv), dq

    (gk, gv), dq = lax.scan(body, (gk, gv), xs)
    return dq, gk, gv


def solution(mesh):
    n = mesh.shape['cp']
    rows = P(('data', 'cp'))
    cols = P(None, ('data', 'cp'))
    perm = [(i, (i + 1) % n) for i in range(n)]

    def local(q, k, v, o, dout, lse):
        c, h, d = q.shape
        scale = d ** -0.5
        me = lax.axis_index('cp')
        xs = _tiles(q, dout, o, lse, n, me)
        base = jnp.arange(c, dtype=jnp.int32) * n
        dq = jnp.zeros((c // TILE, TILE, h, d), jnp.float32)
        gk = jnp.zeros((c, h, d), jnp.float32)
        gv = jnp.zeros((c, h, d), jnp.float32)
        kb, vb = k, v
        for s in range(n):
            kpos = base + (me - s) % n
            dqs, gk, gv = _block_grads(xs, kb, vb, kpos, gk, gv, scale)
            dq = dq + dqs
            if s < n - 1:
                kb = lax.ppermute(kb, 'cp', perm)
                vb = lax.ppermute(vb, 'cp', perm)
            gk = lax.ppermute(gk, 'cp', perm)
            gv = lax.ppermute(gv, 'cp', perm)
        return (dq.reshape(c, h, d).astype(jnp.bfloat16),
                gk.astype(jnp.bfloat16), gv.astype(jnp.bfloat16))

    return jax.shard_map(local, mesh=mesh, in_specs=(rows, rows, rows, rows, rows, cols),
                         out_specs=(rows, rows, rows), check_vma=False)
```

profile of v0, /device:TPU:0, one launch (start us, length us, event | category | flops | bytes accessed | tf_op | source)
XLA Modules:
  0.0 855.1 jit_solution(14632189616787340094)
XLA Ops:
  11.0 41.8 %while.127 = (s32[]{:T(128)}, f32[1024,4,128]{0,2,1:T(8,128)}, f32[1024,4,128]{0,2,1:T(8,128)}, f32[2,512,4,128]{3,1,2,0:T(8,128)}, bf16[2,512,4,128]{3,1,2,0:T(...) while((s32[]{:T(128)}, f32[1024,4,128]{0,2,1:T(8,128)}, ...), condition=%wide.region_1.2_spmd.clone, body=%wide.region_0.1_spmd.clone.sunk | while | flops 2708736000 | bytes 146348896 | solution.py:36
  20.3 4.7 bitcast_add_fusion.46
  40.2 5.3 bitcast_add_fusion.46
  47.8 5.0 bitcast_add_fusion.47
  57.7 55.9 %collective-permute-done.2 = bf16[1024,4,128]{2,0,1:T(8,128)(2,1)} collective-permute-done((bf16[1024,4,128]{2,0,1:T(8,128)(2,1)S(1)}, bf16[1024,4,128]{2,0,1:T(8,128)(2,1)}, u32[]{:S(2)}, u32[]{:S(2)}) %collective-permute-start.2) | collective-permute-done | bytes 1048608 | tf_op jit(solution)/shard_map/ppermute | solution.py:61
  113.6 11.2 %collective-permute-done.3 = bf16[1024,4,128]{2,0,1:T(8,128)(2,1)} collective-permute-done((bf16[1024,4,128]{2,0,1:T(8,128)(2,1)}, bf16[1024,4,128]{2,0,1:T(8,128)(2,1)}, u32[]{:S(2)}, u32[]{:S(2)}) %collective-permute-start.3) | collective-permute-done | bytes 1048608 | tf_op jit(solution)/shard_map/ppermute | solution.py:62
  126.4 39.0 %while.120 = (s32[]{:T(128)}, f32[1024,4,128]{0,2,1:T(8,128)}, f32[1024,4,128]{0,2,1:T(8,128)}, f32[2,512,4,128]{3,1,2,0:T(8,128)}, bf16[2,512,4,128]{3,1,2,0:T(...) while((s32[]{:T(128)}, f32[1024,4,128]{0,2,1:T(8,128)}, ...), condition=%wide.region_3.4_spmd.clone, body=%wide.region_2.3_spmd.clone.sunk | while | flops 2707687424 | bytes 70850776 | solution.py:36
  129.3 4.5 multiply_convert_fusion.16
  136.3 4.6 bitcast_add_fusion.32
  140.9 4.9 bitcast_add_fusion.33
  148.8 4.5 multiply_convert_fusion.16
  155.8 4.6 bitcast_add_fusion.32
  160.5 4.9 bitcast_add_fusion.33
  169.6 55.9 %collective-permute-done.6 = bf16[1024,4,128]{2,0,1:T(8,128)(2,1)S(1)} collective-permute-done((bf16[1024,4,128]{2,0,1:T(8,128)(2,1)}, bf16[1024,4,128]{2,0,1:T(8,128)(2,1)S(1)}, u32[]{:S(2)}, u32[]{:S(2)}) %collective-permute-start.6) | collective-permute-done | bytes 1048608 | tf_op jit(solution)/shard_map/ppermute | solution.py:61
  225.5 11.2 %collective-permute-done.7 = bf16[1024,4,128]{2,0,1:T(8,128)(2,1)} collective-permute-done((bf16[1024,4,128]{2,0,1:T(8,128)(2,1)}, bf16[1024,4,128]{2,0,1:T(8,128)(2,1)}, u32[]{:S(2)}, u32[]{:S(2)}) %collective-permute-start.7) | collective-permute-done | bytes 1048608 | tf_op jit(solution)/shard_map/ppermute | solution.py:62
  238.3 34.3 %while.121 = (s32[]{:T(128)}, f32[1024,4,128]{0,2,1:T(8,128)}, f32[1024,4,128]{0,2,1:T(8,128)}, f32[2,512,4,128]{3,1,2,0:T(8,128)}, bf16[2,512,4,128]{3,1,2,0:T(...) while((s32[]{:T(128)}, f32[1024,4,128]{0,2,1:T(8,128)}, ...), condition=%wide.region_5.6_spmd.clone, body=%wide.region_4.5_spmd.clone.sunk | while | flops 2707687424 | bytes 70850776 | solution.py:36
  245.8 4.7 bitcast_add_fusion.34
  250.4 5.0 bitcast_add_fusion.35
  262.9 4.7 bitcast_add_fusion.34
  267.6 5.0 bitcast_add_fusion.35
  277.0 55.6 %collective-permute-done.10 = bf16[1024,4,128]{2,0,1:T(8,128)(2,1)} collective-permute-done((bf16[1024,4,128]{2,0,1:T(8,128)(2,1)S(1)}, bf16[1024,4,128]{2,0,1:T(8,128)(2,1)}, u32[]{:S(2)}, u32[]{:S(2)}) %collective-permute-start.10) | collective-permute-done | bytes 1048608 | tf_op jit(solution)/shard_map/ppermute | solution.py:61
  332.7 11.2 %collective-permute-done.11 = bf16[1024,4,128]{2,0,1:T(8,128)(2,1)} collective-permute-done((bf16[1024,4,128]{2,0,1:T(8,128)(2,1)}, bf16[1024,4,128]{2,0,1:T(8,128)(2,1)}, u32[]{:S(2)}, u32[]{:S(2)}) %collective-permute-start.11) | collective-permute-done | bytes 1048608 | tf_op jit(solution)/shard_map/ppermute | solution.py:62
  345.4 39.0 %while.122 = (s32[]{:T(128)}, f32[1024,4,128]{0,2,1:T(8,128)}, f32[1024,4,128]{0,2,1:T(8,128)}, f32[2,512,4,128]{3,1,2,0:T(8,128)}, bf16[2,512,4,128]{3,1,2,0:T(...) while((s32[]{:T(128)}, f32[1024,4,128]{0,2,1:T(8,128)}, ...), condition=%wide.region_7.8_spmd.clone, body=%wide.region_6.7_spmd.clone.sunk | while | flops 2707687424 | bytes 70850776 | solution.py:36
  348.3 4.5 multiply_convert_fusion.18
  355.3 4.6 bitcast_add_fusion.36
  360.0 4.9 bitcast_add_fusion.37
  367.8 4.5 multiply_convert_fusion.18
  374.9 4.6 bitcast_add_fusion.36
  379.5 4.9 bitcast_add_fusion.37
  388.6 55.9 %collective-permute-done.14 = bf16[1024,4,128]{2,0,1:T(8,128)(2,1)S(1)} collective-permute-done((bf16[1024,4,128]{2,0,1:T(8,128)(2,1)}, bf16[1024,4,128]{2,0,1:T(8,128)(2,1)S(1)}, u32[]{:S(2)}, u32[]{:S(2)}) %collective-permute-start.14) | collective-permute-done | bytes 1048608 | tf_op jit(solution)/shard_map/ppermute | solution.py:61
  444.5 11.2 %collective-permute-done.15 = bf16[1024,4,128]{2,0,1:T(8,128)(2,1)} collective-permute-done((bf16[1024,4,128]{2,0,1:T(8,128)(2,1)}, bf16[1024,4,128]{2,0,1:T(8,128)(2,1)}, u32[]{:S(2)}, u32[]{:S(2)}) %collective-permute-start.15) | collective-permute-done | bytes 1048608 | tf_op jit(solution)/shard_map/ppermute | solution.py:62
  457.2 34.3 %while.123 = (s32[]{:T(128)}, f32[1024,4,128]{0,2,1:T(8,128)}, f32[1024,4,128]{0,2,1:T(8,128)}, f32[2,512,4,128]{3,1,2,0:T(8,128)}, bf16[2,512,4,128]{3,1,2,0:T(...) while((s32[]{:T(128)}, f32[1024,4,128]{0,2,1:T(8,128)}, ...), condition=%wide.region_9.10_spmd.clone, body=%wide.region_8.9_spmd.clone.sunk | while | flops 2707687424 | bytes 70850776 | solution.py:36
  464.7 4.7 bitcast_add_fusion.38
  469.4 5.0 bitcast_add_fusion.39
  481.9 4.7 bitcast_add_fusion.38
  486.5 5.0 bitcast_add_fusion.39
  495.7 55.9 %collective-permute-done.18 = bf16[1024,4,128]{2,0,1:T(8,128)(2,1)} collective-permute-done((bf16[1024,4,128]{2,0,1:T(8,128)(2,1)S(1)}, bf16[1024,4,128]{2,0,1:T(8,128)(2,1)}, u32[]{:S(2)}, u32[]{:S(2)}) %collective-permute-start.18) | collective-permute-done | bytes 1048608 | tf_op jit(solution)/shard_map/ppermute | solution.py:61
  551.6 11.2 %collective-permute-done.19 = bf16[1024,4,128]{2,0,1:T(8,128)(2,1)} collective-permute-done((bf16[1024,4,128]{2,0,1:T(8,128)(2,1)}, bf16[1024,4,128]{2,0,1:T(8,128)(2,1)}, u32[]{:S(2)}, u32[]{:S(2)}) %collective-permute-start.19) | collective-permute-done | bytes 1048608 | tf_op jit(solution)/shard_map/ppermute | solution.py:62
  564.4 39.0 %while.124 = (s32[]{:T(128)}, f32[1024,4,128]{0,2,1:T(8,128)}, f32[1024,4,128]{0,2,1:T(8,128)}, f32[2,512,4,128]{3,1,2,0:T(8,128)}, bf16[2,512,4,128]{3,1,2,0:T(...) while((s32[]{:T(128)}, f32[1024,4,128]{0,2,1:T(8,128)}, ...), condition=%wide.region_11.12_spmd.clone, body=%wide.region_10.11_spmd.clone.sunk | while | flops 2707687424 | bytes 70850776 | solution.py:36
  567.3 4.5 multiply_convert_fusion.20
  574.3 4.6 bitcast_add_fusion.40
  579.0 4.9 bitcast_add_fusion.41
  586.8 4.5 multiply_convert_fusion.20
  593.8 4.6 bitcast_add_fusion.40
  598.5 4.9 bitcast_add_fusion.41
  607.6 55.9 %collective-permute-done.22 = bf16[1024,4,128]{2,0,1:T(8,128)(2,1)S(1)} collective-permute-done((bf16[1024,4,128]{2,0,1:T(8,128)(2,1)}, bf16[1024,4,128]{2,0,1:T(8,128)(2,1)S(1)}, u32[]{:S(2)}, u32[]{:S(2)}) %collective-permute-start.22) | collective-permute-done | bytes 1048608 | tf_op jit(solution)/shard_map/ppermute | solution.py:61
  663.5 11.2 %collective-permute-done.23 = bf16[1024,4,128]{2,0,1:T(8,128)(2,1)} collective-permute-done((bf16[1024,4,128]{2,0,1:T(8,128)(2,1)}, bf16[1024,4,128]{2,0,1:T(8,128)(2,1)}, u32[]{:S(2)}, u32[]{:S(2)}) %collective-permute-start.23) | collective-permute-done | bytes 1048608 | tf_op jit(solution)/shard_map/ppermute | solution.py:62
  676.3 34.3 %while.125 = (s32[]{:T(128)}, f32[1024,4,128]{0,2,1:T(8,128)}, f32[1024,4,128]{0,2,1:T(8,128)}, f32[2,512,4,128]{3,1,2,0:T(8,128)}, bf16[2,512,4,128]{3,1,2,0:T(...) while((s32[]{:T(128)}, f32[1024,4,128]{0,2,1:T(8,128)}, ...), condition=%wide.region_13.14_spmd.clone, body=%wide.region_12.13_spmd.clone.sunk | while | flops 2707687424 | bytes 70850776 | solution.py:36
  677.9 4.5 multiply_convert_fusion.21
  683.7 4.7 bitcast_add_fusion.42
  688.4 5.0 bitcast_add_fusion.43
  695.1 4.5 multiply_convert_fusion.21
  700.9 4.7 bitcast_add_fusion.42
  705.6 5.0 bitcast_add_fusion.43
  714.8 55.8 %collective-permute-done.26 = bf16[1024,4,128]{2,0,1:T(8,128)(2,1)} collective-permute-done((bf16[1024,4,128]{2,0,1:T(8,128)(2,1)S(1)}, bf16[1024,4,128]{2,0,1:T(8,128)(2,1)}, u32[]{:S(2)}, u32[]{:S(2)}) %collective-permute-start.26) | collective-permute-done | bytes 1048608 | tf_op jit(solution)/shard_map/ppermute | solution.py:61
  770.7 11.2 %collective-permute-done.27 = bf16[1024,4,128]{2,0,1:T(8,128)(2,1)} collective-permute-done((bf16[1024,4,128]{2,0,1:T(8,128)(2,1)}, bf16[1024,4,128]{2,0,1:T(8,128)(2,1)}, u32[]{:S(2)}, u32[]{:S(2)}) %collective-permute-start.27) | collective-permute-done | bytes 1048608 | tf_op jit(solution)/shard_map/ppermute | solution.py:62
  783.4 39.0 %while.126 = (s32[]{:T(128)}, f32[1024,4,128]{0,2,1:T(8,128)}, f32[1024,4,128]{0,2,1:T(8,128)}, f32[2,512,4,128]{3,1,2,0:T(8,128)}, bf16[2,512,4,128]{3,1,2,0:T(...) while((s32[]{:T(128)}, f32[1024,4,128]{0,2,1:T(8,128)}, ...), condition=%wide.region_15.16_spmd.clone, body=%wide.region_14.15_spmd.clone.sunk | while | flops 2707687424 | bytes 70850776 | solution.py:36
  786.3 4.5 multiply_convert_fusion.22
  793.4 4.6 bitcast_add_fusion.44
  798.0 4.9 bitcast_add_fusion.45
  812.9 4.6 bitcast_add_fusion.44
  817.5 4.9 bitcast_add_fusion.45
  827.5 6.3 add_convert_fusion
  839.9 11.2 %collective-permute-done.29 = bf16[1024,4,128]{2,1,0:T(4,128)(2,1)S(1)} collective-permute-done((bf16[1024,4,128]{2,1,0:T(4,128)(2,1)}, bf16[1024,4,128]{2,1,0:T(4,128)(2,1)S(1)}, u32[]{:S(2)}, u32[]{:S(2)}) %collective-permute-start.29) | collective-permute-done | bytes 1048608 | tf_op jit(solution)/shard_map/ppermute | solution.py:64
  (261 shorter events, 175.4 us)
Async XLA Ops:
  2.5 8.5 copy-start.20
  11.0 4.8 copy-start.23
  20.3 4.7 copy-start
  20.3 7.0 copy-start.2
  31.0 4.8 copy-start.23
  40.2 5.3 copy-start
  40.2 7.6 copy-start.2
  52.8 72.1 %collective-permute-start = (f32[1024,4,128]{0,2,1:T(8,128)}, f32[1024,4,128]{0,2,1:T(8,128)}, u32[]{:S(2)}, u32[]{:S(2)}) collective-permute-start(f32[1024,4,128]{0,2,1:T(8,128)} %get-tuple-element.516), channel_id=1, source_target_pairs={{0,1},{1,2},{2,3},{3,4},{4,5},{5,6},{6,7},{7,0},{8,9},{9,10},{10,1... | collective-permute-start | bytes 6291464 | tf_op jit(solution)/shard_map/ppermute | solution.py:63
  53.3 71.5 %collective-permute-start.1 = (f32[1024,4,128]{0,2,1:T(8,128)}, f32[1024,4,128]{0,2,1:T(8,128)}, u32[]{:S(2)}, u32[]{:S(2)}) collective-permute-start(f32[1024,4,128]{0,2,1:T(8,128)} %get-tuple-element.517), channel_id=1, source_target_pairs={{0,1},{1,2},{2,3},{3,4},{4,5},{5,6},{6,7},{7,0},{8,9},{9,10},{10,1... | collective-permute-start | bytes 6291464 | tf_op jit(solution)/shard_map/ppermute | solution.py:64
  55.9 57.7 %collective-permute-start.2 = (bf16[1024,4,128]{2,0,1:T(8,128)(2,1)S(1)}, bf16[1024,4,128]{2,0,1:T(8,128)(2,1)}, u32[]{:S(2)}, u32[]{:S(2)}) collective-permute-start(bf16[1024,4,128]{2,0,1:T(8,128)(2,1)S(1)} %get-tuple-element.2038), channel_id=1, source_target_pairs={{0,1},{1,2},{2,3},{3,4},{4,5},{5,6},{6,7},{7,0},{8,9},{9,10},{10,1... | collective-permute-start | bytes 3145736 | tf_op jit(solution)/shard_map/ppermute | solution.py:61
  56.0 68.9 %collective-permute-start.3 = (bf16[1024,4,128]{2,0,1:T(8,128)(2,1)}, bf16[1024,4,128]{2,0,1:T(8,128)(2,1)}, u32[]{:S(2)}, u32[]{:S(2)}) collective-permute-start(bf16[1024,4,128]{2,0,1:T(8,128)(2,1)} %get-tuple-element.2072), channel_id=1, source_target_pairs={{0,1},{1,2},{2,3},{3,4},{4,5},{5,6},{6,7},{7,0},{8,9},{9,10},{10,1... | collective-permute-start | bytes 3145736 | tf_op jit(solution)/shard_map/ppermute | solution.py:62
  129.3 4.5 copy-start.8
  136.3 4.7 copy-start.9
  148.8 4.5 copy-start.8
  155.8 4.7 copy-start.9
  165.4 71.3 %collective-permute-start.4 = (f32[1024,4,128]{0,2,1:T(8,128)}, f32[1024,4,128]{0,2,1:T(8,128)}, u32[]{:S(2)}, u32[]{:S(2)}) collective-permute-start(f32[1024,4,128]{0,2,1:T(8,128)} %get-tuple-element.519), channel_id=1, source_target_pairs={{0,1},{1,2},{2,3},{3,4},{4,5},{5,6},{6,7},{7,0},{8,9},{9,10},{10,1... | collective-permute-start | bytes 6291464 | tf_op jit(solution)/shard_map/ppermute | solution.py:63
  165.4 71.3 %collective-permute-start.5 = (f32[1024,4,128]{0,2,1:T(8,128)}, f32[1024,4,128]{0,2,1:T(8,128)}, u32[]{:S(2)}, u32[]{:S(2)}) collective-permute-start(f32[1024,4,128]{0,2,1:T(8,128)} %get-tuple-element.520), channel_id=1, source_target_pairs={{0,1},{1,2},{2,3},{3,4},{4,5},{5,6},{6,7},{7,0},{8,9},{9,10},{10,1... | collective-permute-start | bytes 6291464 | tf_op jit(solution)/shard_map/ppermute | solution.py:64
  166.9 58.6 %collective-permute-start.6 = (bf16[1024,4,128]{2,0,1:T(8,128)(2,1)}, bf16[1024,4,128]{2,0,1:T(8,128)(2,1)S(1)}, u32[]{:S(2)}, u32[]{:S(2)}) collective-permute-start(bf16[1024,4,128]{2,0,1:T(8,128)(2,1)} %collective-permute-done.2), channel_id=1, source_target_pairs={{0,1},{1,2},{2,3},{3,4},{4,5},{5,6},{6,7},{7,0},{8,9},{9,10},{10,1... | collective-permute-start | bytes 3145736 | tf_op jit(solution)/shard_map/ppermute | solution.py:61
  166.9 69.8 %collective-permute-start.7 = (bf16[1024,4,128]{2,0,1:T(8,128)(2,1)}, bf16[1024,4,128]{2,0,1:T(8,128)(2,1)}, u32[]{:S(2)}, u32[]{:S(2)}) collective-permute-start(bf16[1024,4,128]{2,0,1:T(8,128)(2,1)} %collective-permute-done.3), channel_id=1, source_target_pairs={{0,1},{1,2},{2,3},{3,4},{4,5},{5,6},{6,7},{7,0},{8,9},{9,10},{10,1... | collective-permute-start | bytes 3145736 | tf_op jit(solution)/shard_map/ppermute | solution.py:62
  240.0 4.5 copy-start.10
  245.8 4.7 copy-start.11
  257.1 4.5 copy-start.10
  262.9 4.7 copy-start.11
  272.6 71.3 %collective-permute-start.8 = (f32[1024,4,128]{0,2,1:T(8,128)}, f32[1024,4,128]{0,2,1:T(8,128)}, u32[]{:S(2)}, u32[]{:S(2)}) collective-permute-start(f32[1024,4,128]{0,2,1:T(8,128)} %get-tuple-element.522), channel_id=1, source_target_pairs={{0,1},{1,2},{2,3},{3,4},{4,5},{5,6},{6,7},{7,0},{8,9},{9,10},{10,1... | collective-permute-start | bytes 6291464 | tf_op jit(solution)/shard_map/ppermute | solution.py:63
  272.6 71.3 %collective-permute-start.9 = (f32[1024,4,128]{0,2,1:T(8,128)}, f32[1024,4,128]{0,2,1:T(8,128)}, u32[]{:S(2)}, u32[]{:S(2)}) collective-permute-start(f32[1024,4,128]{0,2,1:T(8,128)} %get-tuple-element.523), channel_id=1, source_target_pairs={{0,1},{1,2},{2,3},{3,4},{4,5},{5,6},{6,7},{7,0},{8,9},{9,10},{10,1... | collective-permute-start | bytes 6291464 | tf_op jit(solution)/shard_map/ppermute | solution.py:64
  273.2 59.5 %collective-permute-start.10 = (bf16[1024,4,128]{2,0,1:T(8,128)(2,1)S(1)}, bf16[1024,4,128]{2,0,1:T(8,128)(2,1)}, u32[]{:S(2)}, u32[]{:S(2)}) collective-permute-start(bf16[1024,4,128]{2,0,1:T(8,128)(2,1)S(1)} %get-tuple-element.2044), channel_id=1, source_target_pairs={{0,1},{1,2},{2,3},{3,4},{4,5},{5,6},{6,7},{7,0},{8,9},{9,10},{10,1... | collective-permute-start | bytes 3145736 | tf_op jit(solution)/shard_map/ppermute | solution.py:61
  273.2 70.7 %collective-permute-start.11 = (bf16[1024,4,128]{2,0,1:T(8,128)(2,1)}, bf16[1024,4,128]{2,0,1:T(8,128)(2,1)}, u32[]{:S(2)}, u32[]{:S(2)}) collective-permute-start(bf16[1024,4,128]{2,0,1:T(8,128)(2,1)} %collective-permute-done.7), channel_id=1, source_target_pairs={{0,1},{1,2},{2,3},{3,4},{4,5},{5,6},{6,7},{7,0},{8,9},{9,10},{10,1... | collective-permute-start | bytes 3145736 | tf_op jit(solution)/shard_map/ppermute | solution.py:62
  348.3 4.5 copy-start.12
  355.3 4.7 copy-start.13
  367.8 4.5 copy-start.12
  374.9 4.7 copy-start.13
  384.5 71.3 %collective-permute-start.12 = (f32[1024,4,128]{0,2,1:T(8,128)}, f32[1024,4,128]{0,2,1:T(8,128)}, u32[]{:S(2)}, u32[]{:S(2)}) collective-permute-start(f32[1024,4,128]{0,2,1:T(8,128)} %get-tuple-element.525), channel_id=1, source_target_pairs={{0,1},{1,2},{2,3},{3,4},{4,5},{5,6},{6,7},{7,0},{8,9},{9,10},{10,1... | collective-permute-start | bytes 6291464 | tf_op jit(solution)/shard_map/ppermute | solution.py:63
  384.5 71.3 %collective-permute-start.13 = (f32[1024,4,128]{0,2,1:T(8,128)}, f32[1024,4,128]{0,2,1:T(8,128)}, u32[]{:S(2)}, u32[]{:S(2)}) collective-permute-start(f32[1024,4,128]{0,2,1:T(8,128)} %get-tuple-element.526), channel_id=1, source_target_pairs={{0,1},{1,2},{2,3},{3,4},{4,5},{5,6},{6,7},{7,0},{8,9},{9,10},{10,1... | collective-permute-start | bytes 6291464 | tf_op jit(solution)/shard_map/ppermute | solution.py:64
  384.5 60.1 %collective-permute-start.14 = (bf16[1024,4,128]{2,0,1:T(8,128)(2,1)}, bf16[1024,4,128]{2,0,1:T(8,128)(2,1)S(1)}, u32[]{:S(2)}, u32[]{:S(2)}) collective-permute-start(bf16[1024,4,128]{2,0,1:T(8,128)(2,1)} %collective-permute-done.10), channel_id=1, source_target_pairs={{0,1},{1,2},{2,3},{3,4},{4,5},{5,6},{6,7},{7,0},{8,9},{9,10},{10,1... | collective-permute-start | bytes 3145736 | tf_op jit(solution)/shard_map/ppermute | solution.py:61
  385.0 70.7 %collective-permute-start.15 = (bf16[1024,4,128]{2,0,1:T(8,128)(2,1)}, bf16[1024,4,128]{2,0,1:T(8,128)(2,1)}, u32[]{:S(2)}, u32[]{:S(2)}) collective-permute-start(bf16[1024,4,128]{2,0,1:T(8,128)(2,1)} %collective-permute-done.11), channel_id=1, source_target_pairs={{0,1},{1,2},{2,3},{3,4},{4,5},{5,6},{6,7},{7,0},{8,9},{9,10},{10,1... | collective-permute-start | bytes 3145736 | tf_op jit(solution)/shard_map/ppermute | solution.py:62
  464.7 4.7 copy-start.15
  481.9 4.7 copy-start.15
  491.6 71.3 %collective-permute-start.16 = (f32[1024,4,128]{0,2,1:T(8,128)}, f32[1024,4,128]{0,2,1:T(8,128)}, u32[]{:S(2)}, u32[]{:S(2)}) collective-permute-start(f32[1024,4,128]{0,2,1:T(8,128)} %get-tuple-element.528), channel_id=1, source_target_pairs={{0,1},{1,2},{2,3},{3,4},{4,5},{5,6},{6,7},{7,0},{8,9},{9,10},{10,1... | collective-permute-start | bytes 6291464 | tf_op jit(solution)/shard_map/ppermute | solution.py:63
  491.6 71.3 %collective-permute-start.17 = (f32[1024,4,128]{0,2,1:T(8,128)}, f32[1024,4,128]{0,2,1:T(8,128)}, u32[]{:S(2)}, u32[]{:S(2)}) collective-permute-start(f32[1024,4,128]{0,2,1:T(8,128)} %get-tuple-element.529), channel_id=1, source_target_pairs={{0,1},{1,2},{2,3},{3,4},{4,5},{5,6},{6,7},{7,0},{8,9},{9,10},{10,1... | collective-permute-start | bytes 6291464 | tf_op jit(solution)/shard_map/ppermute | solution.py:64
  491.6 60.1 %collective-permute-start.18 = (bf16[1024,4,128]{2,0,1:T(8,128)(2,1)S(1)}, bf16[1024,4,128]{2,0,1:T(8,128)(2,1)}, u32[]{:S(2)}, u32[]{:S(2)}) collective-permute-start(bf16[1024,4,128]{2,0,1:T(8,128)(2,1)S(1)} %get-tuple-element.2047), channel_id=1, source_target_pairs={{0,1},{1,2},{2,3},{3,4},{4,5},{5,6},{6,7},{7,0},{8,9},{9,10},{10,1... | collective-permute-start | bytes 3145736 | tf_op jit(solution)/shard_map/ppermute | solution.py:61
  492.1 70.7 %collective-permute-start.19 = (bf16[1024,4,128]{2,0,1:T(8,128)(2,1)}, bf16[1024,4,128]{2,0,1:T(8,128)(2,1)}, u32[]{:S(2)}, u32[]{:S(2)}) collective-permute-start(bf16[1024,4,128]{2,0,1:T(8,128)(2,1)} %collective-permute-done.15), channel_id=1, source_target_pairs={{0,1},{1,2},{2,3},{3,4},{4,5},{5,6},{6,7},{7,0},{8,9},{9,10},{10,1... | collective-permute-start | bytes 3145736 | tf_op jit(solution)/shard_map/ppermute | solution.py:62
  567.3 4.5 copy-start.16
  574.3 4.7 copy-start.17
  586.8 4.5 copy-start.16
  593.8 4.7 copy-start.17
  603.4 71.3 %collective-permute-start.20 = (f32[1024,4,128]{0,2,1:T(8,128)}, f32[1024,4,128]{0,2,1:T(8,128)}, u32[]{:S(2)}, u32[]{:S(2)}) collective-permute-start(f32[1024,4,128]{0,2,1:T(8,128)} %get-tuple-element.531), channel_id=1, source_target_pairs={{0,1},{1,2},{2,3},{3,4},{4,5},{5,6},{6,7},{7,0},{8,9},{9,10},{10,1... | collective-permute-start | bytes 6291464 | tf_op jit(solution)/shard_map/ppermute | solution.py:63
  603.4 71.3 %collective-permute-start.21 = (f32[1024,4,128]{0,2,1:T(8,128)}, f32[1024,4,128]{0,2,1:T(8,128)}, u32[]{:S(2)}, u32[]{:S(2)}) collective-permute-start(f32[1024,4,128]{0,2,1:T(8,128)} %get-tuple-element.532), channel_id=1, source_target_pairs={{0,1},{1,2},{2,3},{3,4},{4,5},{5,6},{6,7},{7,0},{8,9},{9,10},{10,1... | collective-permute-start | bytes 6291464 | tf_op jit(solution)/shard_map/ppermute | solution.py:64
  603.4 60.1 %collective-permute-start.22 = (bf16[1024,4,128]{2,0,1:T(8,128)(2,1)}, bf16[1024,4,128]{2,0,1:T(8,128)(2,1)S(1)}, u32[]{:S(2)}, u32[]{:S(2)}) collective-permute-start(bf16[1024,4,128]{2,0,1:T(8,128)(2,1)} %collective-permute-done.18), channel_id=1, source_target_pairs={{0,1},{1,2},{2,3},{3,4},{4,5},{5,6},{6,7},{7,0},{8,9},{9,10},{10,1... | collective-permute-start | bytes 3145736 | tf_op jit(solution)/shard_map/ppermute | solution.py:61
  604.0 70.7 %collective-permute-start.23 = (bf16[1024,4,128]{2,0,1:T(8,128)(2,1)}, bf16[1024,4,128]{2,0,1:T(8,128)(2,1)}, u32[]{:S(2)}, u32[]{:S(2)}) collective-permute-start(bf16[1024,4,128]{2,0,1:T(8,128)(2,1)} %collective-permute-done.19), channel_id=1, source_target_pairs={{0,1},{1,2},{2,3},{3,4},{4,5},{5,6},{6,7},{7,0},{8,9},{9,10},{10,1... | collective-permute-start | bytes 3145736 | tf_op jit(solution)/shard_map/ppermute | solution.py:62
  677.9 4.5 copy-start.18
  683.7 4.7 copy-start.19
  695.1 4.5 copy-start.18
  700.9 4.7 copy-start.19
  710.6 71.3 %collective-permute-start.24 = (f32[1024,4,128]{0,2,1:T(8,128)}, f32[1024,4,128]{0,2,1:T(8,128)}, u32[]{:S(2)}, u32[]{:S(2)}) collective-permute-start(f32[1024,4,128]{0,2,1:T(8,128)} %get-tuple-element.534), channel_id=1, source_target_pairs={{0,1},{1,2},{2,3},{3,4},{4,5},{5,6},{6,7},{7,0},{8,9},{9,10},{10,1... | collective-permute-start | bytes 6291464 | tf_op jit(solution)/shard_map/ppermute | solution.py:63
  710.6 71.3 %collective-permute-start.25 = (f32[1024,4,128]{0,2,1:T(8,128)}, f32[1024,4,128]{0,2,1:T(8,128)}, u32[]{:S(2)}, u32[]{:S(2)}) collective-permute-start(f32[1024,4,128]{0,2,1:T(8,128)} %get-tuple-element.535), channel_id=1, source_target_pairs={{0,1},{1,2},{2,3},{3,4},{4,5},{5,6},{6,7},{7,0},{8,9},{9,10},{10,1... | collective-permute-start | bytes 6291464 | tf_op jit(solution)/shard_map/ppermute | solution.py:64
  710.6 60.1 %collective-permute-start.26 = (bf16[1024,4,128]{2,0,1:T(8,128)(2,1)S(1)}, bf16[1024,4,128]{2,0,1:T(8,128)(2,1)}, u32[]{:S(2)}, u32[]{:S(2)}) collective-permute-start(bf16[1024,4,128]{2,0,1:T(8,128)(2,1)S(1)} %get-tuple-element.2041), channel_id=1, source_target_pairs={{0,1},{1,2},{2,3},{3,4},{4,5},{5,6},{6,7},{7,0},{8,9},{9,10},{10,1... | collective-permute-start | bytes 3145736 | tf_op jit(solution)/shard_map/ppermute | solution.py:61
  711.2 70.7 %collective-permute-start.27 = (bf16[1024,4,128]{2,0,1:T(8,128)(2,1)}, bf16[1024,4,128]{2,0,1:T(8,128)(2,1)}, u32[]{:S(2)}, u32[]{:S(2)}) collective-permute-start(bf16[1024,4,128]{2,0,1:T(8,128)(2,1)} %collective-permute-done.23), channel_id=1, source_target_pairs={{0,1},{1,2},{2,3},{3,4},{4,5},{5,6},{6,7},{7,0},{8,9},{9,10},{10,1... | collective-permute-start | bytes 3145736 | tf_op jit(solution)/shard_map/ppermute | solution.py:62
  786.3 4.5 copy-start.5
  793.4 4.7 copy-start.6
  805.8 4.5 copy-start.5
  812.9 4.7 copy-start.6
  822.5 5.1 copy-start.7
  824.7 15.2 %collective-permute-start.28 = (bf16[1024,4,128]{2,1,0:T(4,128)(2,1)S(1)}, bf16[1024,4,128]{2,1,0:T(4,128)(2,1)}, u32[]{:S(2)}, u32[]{:S(2)}) collective-permute-start(bf16[1024,4,128]{2,1,0:T(4,128)(2,1)S(1)} %copy.71), channel_id=1, source_target_pairs={{0,1},{1,2},{2,3},{3,4},{4,5},{5,6},{6,7},{7,0},{8,9},{9,10},{10,1... | collective-permute-start | bytes 3145736 | tf_op jit(solution)/shard_map/ppermute | solution.py:63
  827.5 23.6 %collective-permute-start.29 = (bf16[1024,4,128]{2,1,0:T(4,128)(2,1)}, bf16[1024,4,128]{2,1,0:T(4,128)(2,1)S(1)}, u32[]{:S(2)}, u32[]{:S(2)}) collective-permute-start(bf16[1024,4,128]{2,1,0:T(4,128)(2,1)} %copy.72), channel_id=1, source_target_pairs={{0,1},{1,2},{2,3},{3,4},{4,5},{5,6},{6,7},{7,0},{8,9},{9,10},{10,1... | collective-permute-start | bytes 3145736 | tf_op jit(solution)/shard_map/ppermute | solution.py:64
  (10 other events, 30.0 us)
where the time goes:
time: 864 us; the launch traced here: 855 us
  waiting for transfers between devices  485 us (56%)
  matrix products  287 us (33%)
  local copies, waits for them, and re-layouts  35.9 us (4%)
  starting transfers between devices  30.3 us (4%)
  other arithmetic  14.1 us (2%)
    ppermute x7, waiting for transfers between devices, local(): kb = lax.ppermute(kb, 'cp', perm)  391 us
    ppermute x7, waiting for transfers between devices, local(): vb = lax.ppermute(vb, 'cp', perm)  78.6 us
    dot_general x16, matrix products, body(): jnp.einsum('hqk,qhd->khd', p.astype(jnp.bfloat16), dt, preferred_element_...  78.4 us
    dot_general x16, matrix products, body(): jnp.einsum('hqk,qhd->khd', ds, qt, preferred_element_type=f32) * scale  75.1 us
    dot_general x16, matrix products, body(): dp = jnp.einsum('qhd,khd->hqk', dt, vb, preferred_element_type=f32)  71.8 us
    dot_general x16, matrix products, body(): dq = jnp.einsum('hqk,khd->qhd', ds, kb, preferred_element_type=f32) * scale  32.1 us
    dot_general x16, matrix products, body(): s = jnp.einsum('qhd,khd->hqk', qt, kb, preferred_element_type=f32) * scale  29.8 us
    ppermute x7, starting transfers between devices, local(): vb = lax.ppermute(vb, 'cp', perm)  22.8 us
  transfers between devices with their start and end apart: 30, of which 16 were waited for; matrix products, arithmetic and copies ran while one was open for 1% of the time, Pallas kernels for 0%

commit v1 on v0

v1 whole, which is shorter than its diff:
```python
import functools
import math

import jax
import jax.numpy as jnp
from jax import lax
from jax.experimental import pallas as pl
from jax.experimental.pallas import tpu as pltpu
from jax.sharding import PartitionSpec as P

MESH = pl.DeviceIdType.MESH
F32 = jnp.float32
BF16 = jnp.bfloat16
ROWS = 128
LOG2E = math.log2(math.e)


def _dot(a, b, ca, cb):
    return lax.dot_general(a, b, (((ca,), (cb,)), ((), ())), preferred_element_type=F32)


def _kernel(nb, x, aux, out, rx, rs, axr, kt, dk, dv, dqt, dqp, okv, oq,
            in_s, in_r, in_l, fw_s, fw_r, ax_s, ax_r, ax_l, kv_s, kv_r, kv_l,
            qp_s, qp_r, oq_s, oq_r, oq_l):
    hd = x.shape[-1]
    tile = 4 * ROWS
    scale = hd ** -0.5
    me = lax.axis_index('cp')
    core = me % 2
    chip = me // 2
    cx, cy = chip % 2, chip // 2
    sib = chip * 2 + (1 - core)
    rel = [cy * 2 + (1 - cx), (1 - cy) * 2 + cx, 3 - chip]

    barrier = pltpu.get_barrier_semaphore()
    for t in range(1, 8):
        pl.semaphore_signal(barrier, inc=1, device_id={'cp': (me + t) % 8}, device_id_type=MESH)
    pl.semaphore_wait(barrier, 7)

    def remote(src, dst, ss, rsem, dev):
        return pltpu.make_async_remote_copy(src_ref=src, dst_ref=dst, send_sem=ss, recv_sem=rsem,
                                            device_id={'cp': dev}, device_id_type=MESH)

    def rows(b):
        return pl.ds(pl.multiple_of(b * ROWS, ROWS), ROWS)

    def aux_send(t):
        dev = (me + t) % 8
        return remote(aux.at[dev // 2], axr.at[core, chip], ax_s.at[t - 1], ax_r.at[t - 1], dev)

    def aux_recv(t):
        dev = (me + 8 - t) % 8
        return remote(aux.at[0], axr.at[dev % 2, dev // 2], ax_s.at[t - 1], ax_r.at[t - 1], dev)

    def in_send(b, d):
        return remote(x.at[:, rel[d], rows(b)], rx.at[b, chip], in_s.at[b, d], in_r.at[b, d], rel[d] * 2 + core)

    def in_recv(b, d):
        return remote(x.at[:, 0, rows(b)], rx.at[b, rel[d]], in_s.at[b, d], in_r.at[b, d], rel[d] * 2 + core)

    def in_local(b):
        return pltpu.make_async_copy(x.at[:, chip, rows(b)], rx.at[b, chip], in_l.at[b])

    def forward(b):
        return remote(rx.at[b, :, 0:2], rs.at[b], fw_s.at[b], fw_r.at[b], sib)

    def kv_send(b, d):
        return remote(okv.at[b, :, rel[d]], out.at[1:3, chip, rows(b)], kv_s.at[b, d], kv_r.at[b, d], rel[d] * 2 + core)

    def kv_recv(b, d):
        return remote(okv.at[b, :, rel[d]], out.at[1:3, rel[d], rows(b)], kv_s.at[b, d], kv_r.at[b, d], rel[d] * 2 + core)

    def kv_local(b):
        return pltpu.make_async_copy(okv.at[b, :, chip], out.at[1:3, chip, rows(b)], kv_l.at[b])

    def part_send(b):
        return remote(dqt.at[1, b], dqp.at[b], qp_s.at[b], qp_r.at[b], sib)

    def q_send(b, d):
        return remote(oq.at[b, rel[d]], out.at[0, chip, rows(b)], oq_s.at[b, d], oq_r.at[b, d], rel[d] * 2 + core)

    def q_recv(b, d):
        return remote(oq.at[b, rel[d]], out.at[0, rel[d], rows(b)], oq_s.at[b, d], oq_r.at[b, d], rel[d] * 2 + core)

    def q_local(b):
        return pltpu.make_async_copy(oq.at[b, chip], out.at[0, chip, rows(b)], oq_l.at[b])

    own_aux = pltpu.make_async_copy(aux.at[chip], axr.at[core, chip], ax_l.at[0])
    own_aux.start()
    for t in range(1, 8):
        aux_send(t).start()

    def issue(n, c):
        b = nb - 1 - n
        in_local(b).start()
        for d in (2, 0, 1):
            in_send(b, d).start()
        return c

    lax.fori_loop(0, nb, issue, 0)
    own_aux.wait()
    for t in range(1, 8):
        aux_recv(t).wait_recv()

    kidx = lax.broadcasted_iota(jnp.int32, (tile, 1), 0)
    qidx = lax.broadcasted_iota(jnp.int32, (1, tile), 1)
    kpos = (kidx % ROWS) * 8 + (kidx // ROWS) * 2 + core

    def pair(b, qb, other, diag, fresh=False):
        if other:
            q = rs[qb, :, 0].reshape(tile, hd)
            do = rs[qb, :, 1].reshape(tile, hd)
            par = 1 - core
        else:
            q = rx[qb, :, 0].reshape(tile, hd)
            do = rx[qb, :, 1].reshape(tile, hd)
            par = core
        k = rx[b, :, 2].reshape(tile, hd)
        v = rx[b, :, 3].reshape(tile, hd)
        lse = jnp.concatenate([axr[par, i, qb] for i in range(4)], axis=1)
        dd = jnp.concatenate([axr[par, i, qb + nb] for i in range(4)], axis=1)
        s = _dot(k, q, 1, 1)
        p = jnp.exp2(s * (scale * LOG2E) - lse)
        if diag:
            qpos = (qidx % ROWS) * 8 + (qidx // ROWS) * 2 + par
            p = jnp.where(kpos <= qpos, p, 0.0)
        dp = _dot(v, do, 1, 1)
        ds = (p * (dp - dd)).astype(BF16)
        gv = _dot(p.astype(BF16), do, 1, 0)
        gk = _dot(ds, q, 1, 0)
        gq = _dot(kt[...], ds, 1, 0)
        if fresh:
            dv[...] = gv
            dk[...] = gk
        else:
            dv[...] += gv
            dk[...] += gk
        if diag:
            dqt[int(other), qb] = gq
        else:
            dqt[int(other), qb] += gq

    def arrive(b):
        for d in range(3):
            in_recv(b, d).wait_recv()
        in_local(b).wait()
        forward(b).start()
        kt[...] = rx[b, :, 2].reshape(tile, hd).astype(F32).T.astype(BF16)

    def emit_kv(b):
        okv[b, 0] = (dk[...] * scale).astype(BF16).reshape(4, ROWS, hd)
        okv[b, 1] = dv[...].astype(BF16).reshape(4, ROWS, hd)
        kv_local(b).start()
        for d in (2, 0, 1):
            kv_send(b, d).start()

    def step(n, c):
        b = nb - 1 - n
        arrive(b)
        pair(b, b, False, True, fresh=True)

        def own(i, c):
            pair(b, i, False, False)
            return c

        lax.fori_loop(b + 1, nb, own, 0)
        forward(b).wait_recv()
        pair(b, b, True, True)

        def oth(i, c):
            pair(b, i, True, False)
            return c

        lax.fori_loop(b + 1, nb, oth, 0)
        emit_kv(b)
        return c

    lax.fori_loop(0, nb - 1, step, 0)

    arrive(0)
    dv[...] = jnp.zeros_like(dv)
    dk[...] = jnp.zeros_like(dk)

    def finish(i):
        part_send(i).wait_recv()
        g = (dqt[0, i] + dqp[i]) * scale
        oq[i] = g.T.astype(BF16).reshape(4, ROWS, hd)
        q_local(i).start()
        for d in (2, 0, 1):
            q_send(i, d).start()

    def last_oth(n, c):
        i = nb - 1 - n
        pair(0, i, True, False)
        part_send(i).start()
        return c

    lax.fori_loop(0, nb - 1, last_oth, 0)
    forward(0).wait_recv()
    pair(0, 0, True, True)
    part_send(0).start()

    def last_own(n, c):
        i = nb - 1 - n
        pair(0, i, False, False)
        finish(i)
        return c

    lax.fori_loop(0, nb - 1, last_own, 0)
    pair(0, 0, False, True)
    emit_kv(0)
    finish(0)

    for t in range(1, 8):
        aux_send(t).wait_send()

    def drain(b, c):
        for d in range(3):
            in_send(b, d).wait_send()
            kv_send(b, d).wait_send()
            kv_recv(b, d).wait_recv()
            q_send(b, d).wait_send()
            q_recv(b, d).wait_recv()
        forward(b).wait_send()
        part_send(b).wait_send()
        kv_local(b).wait()
        q_local(b).wait()
        return c

    lax.fori_loop(0, nb, drain, 0)


def solution(mesh):
    rows = P(('data', 'cp'))
    cols = P(None, ('data', 'cp'))

    def local(q, k, v, o, dout, lse):
        c, h, d = q.shape
        nb = c // ROWS
        dd = jnp.einsum('qhd,qhd->hq', dout, o, preferred_element_type=F32)
        x = jnp.stack([a.transpose(1, 0, 2) for a in (q, dout, k, v)])
        aux = jnp.concatenate([(lse * LOG2E).reshape(h, nb, 1, ROWS), dd.reshape(h, nb, 1, ROWS)], axis=1)
        dma = pltpu.SemaphoreType.DMA
        out = pl.pallas_call(
            functools.partial(_kernel, nb),
            out_shape=jax.ShapeDtypeStruct((3, h, c, d), BF16),
            in_specs=[pl.BlockSpec(memory_space=pl.ANY)] * 2,
            out_specs=pl.BlockSpec(memory_space=pl.ANY),
            scratch_shapes=[
                pltpu.VMEM((nb, 4, 4, ROWS, d), BF16),
                pltpu.VMEM((nb, 4, 2, ROWS, d), BF16),
                pltpu.VMEM((2, 4, 2 * nb, 1, ROWS), F32),
                pltpu.VMEM((d, 4 * ROWS), BF16),
                pltpu.VMEM((4 * ROWS, d), F32),
                pltpu.VMEM((4 * ROWS, d), F32),
                pltpu.VMEM((2, nb, d, 4 * ROWS), F32),
                pltpu.VMEM((nb, d, 4 * ROWS), F32),
                pltpu.VMEM((nb, 2, 4, ROWS, d), BF16),
                pltpu.VMEM((nb, 4, ROWS, d), BF16),
                dma((nb, 3)), dma((nb, 3)), dma((nb,)),
                dma((nb,)), dma((nb,)),
                dma((7,)), dma((7,)), dma((1,)),
                dma((nb, 3)), dma((nb, 3)), dma((nb,)),
                dma((nb,)), dma((nb,)),
                dma((nb, 3)), dma((nb, 3)), dma((nb,)),
            ],
            compiler_params=pltpu.CompilerParams(
                collective_id=0, has_side_effects=True, vmem_limit_bytes=60 << 20),
            name='attn_bwd',
        )(x, aux)
        return tuple(out[i].transpose(1, 0, 2) for i in range(3))

    return jax.shard_map(local, mesh=mesh, in_specs=(rows, rows, rows, rows, rows, cols),
                         out_specs=(rows, rows, rows), check_vma=False)
```

time: 864 us -> 106 us (0.12); the launches traced: 855 us -> 106 us
  waiting for transfers between devices: 485 us -> 0 us
  matrix products: 287 us -> 0 us
  Pallas kernels: 0 us -> 91 us
  starting transfers between devices: 30.3 us -> 0 us
  local copies, waits for them, and re-layouts: 35.9 us -> 10.1 us
  other arithmetic: 14.1 us -> 4.13 us
    ppermute x30 -> x0, waiting for transfers between devices: 485 us -> none  [the longest x7 391 us: local(): kb = lax.ppermute(kb, 'cp', perm)]
    dot_general x80 -> x0, matrix products: 287 us -> none  [the longest x16 78.4 us: body(): jnp.einsum('hqk,qhd->khd', p.astype(jnp.bfloat16), dt, preferred_element_...]
    pallas_call x0 -> x1, Pallas kernels: none -> 91 us  [local(): pl.pallas_call(functools.partial(_kernel, nb), out_shape=jax.ShapeDtypeSt...]
    ppermute x30 -> x0, starting transfers between devices: 30.3 us -> none  [the longest x7 22.8 us: local(): vb = lax.ppermute(vb, 'cp', perm)]
    while x82 -> x0, local copies, waits for them, and re-layouts: 11.4 us -> none
    another operation x8 -> x2, local copies, waits for them, and re-layouts: 12.1 us -> 2.23 us  [local(): x = jnp.stack([a.transpose(1, 0, 2) for a in (q, dout, k, v)])]
  transfers between devices with their start and end apart: 30 -> 0, of which waited for: 16 -> 0; matrix products, arithmetic and copies ran while one was open for 1% -> 0% of each run, Pallas kernels for 0% -> 0%
where the time goes in v1:
time: 106 us
  Pallas kernels  91 us (86%)
  local copies, waits for them, and re-layouts  10.1 us (10%)
  other arithmetic  4.13 us (4%)
    pallas_call x1, Pallas kernels, local(): pl.pallas_call(functools.partial(_kernel, nb), out_shape=jax.ShapeDtypeSt...  91 us
    unnamed x11, local copies, waits for them, and re-layouts  5.54 us
    another operation x2, local copies, waits for them, and re-layouts, local(): x = jnp.stack([a.transpose(1, 0, 2) for a in (q, dout, k, v)])  2.23 us
    another operation x1, other arithmetic, local(): x = jnp.stack([a.transpose(1, 0, 2) for a in (q, dout, k, v)])  2.22 us

profile of v1, /device:TPU:0, one launch (start us, length us, event | category | flops | bytes accessed | tf_op | source)
XLA Modules:
  0.0 105.9 jit_solution(2919864797116243005)
XLA Ops:
  0.6 0.0 copy-start
  0.6 0.0 copy-start.2
  0.7 2.0 %copy_bitcast_fusion = (bf16[1,4,1024,128]{3,2,1,0:T(8,128)(2,1)S(1)}, bf16[1,4,1024,128]{3,2,1,0:T(8,128)(2,1)S(1)}) fusion(bf16[1024,4,128]{2,1,0:T(4,128)(2,1)} %param.8, bf16[1024,4,128]{2,1,0:T(4,128)(2,1)} %param.7), kind=kLoop, calls=%fused_computation.3 | loop fusion | bytes 4194304 | tf_op jit(solution)/shard_map/stack | solution.py:241
  2.6 0.0 copy-done
  2.6 0.2 copy-done.2
  2.8 0.3 copy_bitcast_fusion.2
  3.1 0.0 copy-start.1
  3.1 0.0 copy-start.3
  3.1 2.2 %pad_maximum_fusion.x = bf16[4,4,1024,128]{3,2,1,0:T(8,128)(2,1)} fusion(bf16[1,4,1024,128]{3,2,1,0:T(8,128)(2,1)S(1)} %get-tuple-element.9, bf16[1,4,1024,128]{3,2,1,0:T(8,128)(2,1)S(1)} %get-tuple-element.10, bf16[1,4,1024,128]{3,2,1,0:T(8,128)(2,1)S(1)} %get-tuple-element.11, bf16[1,4,1024,128]{3,2,1,0:T(8,128)(2,1)S(1)} %get-tuple-element.12), kind=kLoop, calls=%fused_computation | loop fusion | flops 6291456 | bytes 8388608 | tf_op jit(solution)/shard_map/stack | solution.py:241
  5.3 0.0 copy-done.1
  5.3 1.2 %fusion = f32[4,1024]{0,1:T(8,128)S(1)} fusion(bf16[1024,4,128]{2,1,0:T(4,128)(2,1)S(1)} %copy-done.1, bf16[1024,4,128]{2,1,0:T(4,128)(2,1)S(1)} %copy-done), kind=kLoop, calls=%fused_computation.2 | loop fusion | flops 2093056 | bytes 2113536
  6.6 0.2 copy.24
  6.8 0.0 copy-done.3
  6.8 0.6 pad_maximum_fusion.1.aux
  7.5 91.0 %attn_bwd.1 = bf16[3,4,1024,128]{3,2,1,0:T(8,128)(2,1)} custom-call(bf16[4,4,1024,128]{3,2,1,0:T(8,128)(2,1)} %pad_maximum_fusion.x, f32[4,16,1,128]{3,2,1,0:T(1,128)} %pad_maximum_fusion.1.aux), custom_call_target="tpu_custom_call" | custom-call | tf_op jit(solution)/shard_map/attn_bwd/pallas_call | solution.py:244
  98.5 2.1 %slice_bitcast_fusion = (bf16[1024,4,128]{2,0,1:T(8,128)(2,1)S(1)}, bf16[1024,4,128]{2,0,1:T(8,128)(2,1)S(1)}, bf16[1024,4,128]{2,0,1:T(8,128)(2,1)S(1)}) fusion(bf16[3,4,1024,128]{3,2,1,0:T(8,128)(2,1)} %attn_bwd.1), kind=kLoop, calls=%fused_computation.7 | loop fusion | bytes 6291456 | tf_op jit(solution)/shard_map/transpose | solution.py:271
  100.5 1.8 %copy.13 = bf16[1024,4,128]{2,1,0:T(4,128)(2,1)} copy(bf16[1024,4,128]{2,0,1:T(8,128)(2,1)S(1)} %get-tuple-element.8) | data formatting | bytes 2097152
  102.3 1.8 %copy.14 = bf16[1024,4,128]{2,1,0:T(4,128)(2,1)} copy(bf16[1024,4,128]{2,0,1:T(8,128)(2,1)S(1)} %get-tuple-element.7) | data formatting | bytes 2097152
  104.1 1.8 %copy.15 = bf16[1024,4,128]{2,1,0:T(4,128)(2,1)} copy(bf16[1024,4,128]{2,0,1:T(8,128)(2,1)S(1)} %get-tuple-element.6) | data formatting | bytes 2097152
  (2 shorter events, 0.0 us)
Async XLA Ops:
  0.6 2.0 %copy-start = (bf16[1024,4,128]{2,1,0:T(4,128)(2,1)S(1)}, bf16[1024,4,128]{2,1,0:T(4,128)(2,1)}, u32[]{:S(2)}) copy-start(bf16[1024,4,128]{2,1,0:T(4,128)(2,1)} %param.10) | copy-start | bytes 3145732
  0.6 2.2 %copy-start.2 = (bf16[1024,4,128]{2,1,0:T(4,128)(2,1)S(1)}, bf16[1024,4,128]{2,1,0:T(4,128)(2,1)}, u32[]{:S(2)}) copy-start(bf16[1024,4,128]{2,1,0:T(4,128)(2,1)} %param.6) | copy-start | bytes 3145732
  3.1 2.2 %copy-start.1 = (bf16[1024,4,128]{2,1,0:T(4,128)(2,1)S(1)}, bf16[1024,4,128]{2,1,0:T(4,128)(2,1)}, u32[]{:S(2)}) copy-start(bf16[1024,4,128]{2,1,0:T(4,128)(2,1)} %param.9) | copy-start | bytes 3145732
  3.1 3.7 %copy-start.3 = (f32[4,1024]{1,0:T(4,128)S(1)}, f32[4,1024]{1,0:T(4,128)}, u32[]{:S(2)}) copy-start(f32[4,1024]{1,0:T(4,128)} %param.11) | copy-start | bytes 49156

commit v2 on v1

v2 whole, which is shorter than its diff:
```python
import functools
import math

import jax
import jax.numpy as jnp
from jax import lax
from jax.experimental import pallas as pl
from jax.experimental.pallas import tpu as pltpu
from jax.sharding import PartitionSpec as P

MESH = pl.DeviceIdType.MESH
F32 = jnp.float32
BF16 = jnp.bfloat16
ROWS = 128
VMEM_LIMIT = 52 << 20
LOG2E = math.log2(math.e)


def _dot(a, b, ca, cb):
    return lax.dot_general(a, b, (((ca,), (cb,)), ((), ())), preferred_element_type=F32)


def _kernel(nb, q_in, do_in, k_in, v_in, o_in, lse_in, dq_out, dk_out, dv_out,
            raw, lsev, xs, auxs, rx, rs, axr, kt, dk, dv, dqt, dqp, okv, oq, orx, ost,
            raw_l, lse_l, in_s, in_r, fw_s, fw_r, ax_s, ax_r, fa_s, fa_r, kv_s, kv_r,
            qp_s, qp_r, oq_s, oq_r, out_l):
    hd = q_in.shape[-1]
    tile = 4 * ROWS
    scale = hd ** -0.5
    me = lax.axis_index('cp')
    core = me % 2
    chip = me // 2
    cx, cy = chip % 2, chip // 2
    sib = chip * 2 + (1 - core)
    rel = [cy * 2 + (1 - cx), (1 - cy) * 2 + cx, 3 - chip]

    def remote(src, dst, ss, rsem, dev):
        return pltpu.make_async_remote_copy(src_ref=src, dst_ref=dst, send_sem=ss, recv_sem=rsem,
                                            device_id={'cp': dev}, device_id_type=MESH)

    def rows(b):
        return pl.ds(pl.multiple_of(b * ROWS, ROWS), ROWS)

    def raw_copy(i, b):
        src = (q_in, do_in, k_in, v_in, o_in)[i]
        return pltpu.make_async_copy(src.at[rows(b)], raw.at[b, i], raw_l.at[b, i])

    def in_send(b, d):
        return remote(xs.at[b, rel[d]], rx.at[b, chip], in_s.at[b, d], in_r.at[b, d], rel[d] * 2 + core)

    def in_recv(b, d):
        return remote(xs.at[b, rel[d]], rx.at[b, rel[d]], in_s.at[b, d], in_r.at[b, d], rel[d] * 2 + core)

    def aux_send(b, d):
        return remote(auxs.at[b, rel[d]], axr.at[b, core, chip], ax_s.at[b, d], ax_r.at[b, d], rel[d] * 2 + core)

    def aux_recv(b, d):
        return remote(auxs.at[b, rel[d]], axr.at[b, core, rel[d]], ax_s.at[b, d], ax_r.at[b, d], rel[d] * 2 + core)

    def forward(b):
        return remote(rx.at[b, :, 0:2], rs.at[b], fw_s.at[b], fw_r.at[b], sib)

    def aux_forward(b):
        return remote(axr.at[b, core], axr.at[b, core], fa_s.at[b], fa_r.at[b], sib)

    def aux_forwarded(b):
        return remote(axr.at[b, core], axr.at[b, 1 - core], fa_s.at[b], fa_r.at[b], sib)

    def kv_send(b, d):
        return remote(okv.at[b, :, rel[d]], orx.at[b, 1:3, chip], kv_s.at[b, d], kv_r.at[b, d], rel[d] * 2 + core)

    def kv_recv(b, d):
        return remote(okv.at[b, :, rel[d]], orx.at[b, 1:3, rel[d]], kv_s.at[b, d], kv_r.at[b, d], rel[d] * 2 + core)

    def part_send(b):
        return remote(dqt.at[1, b], dqp.at[b], qp_s.at[b], qp_r.at[b], sib)

    def q_send(b, d):
        return remote(oq.at[b, rel[d]], orx.at[b, 0, chip], oq_s.at[b, d], oq_r.at[b, d], rel[d] * 2 + core)

    def q_recv(b, d):
        return remote(oq.at[b, rel[d]], orx.at[b, 0, rel[d]], oq_s.at[b, d], oq_r.at[b, d], rel[d] * 2 + core)

    def out_copy(a, b):
        return pltpu.make_async_copy(ost.at[b, a], (dq_out, dk_out, dv_out)[a].at[rows(b)], out_l.at[b, a])

    lse_copy = pltpu.make_async_copy(lse_in, lsev, lse_l.at[0])
    lse_copy.start()

    def load(n, c):
        for i in range(5):
            raw_copy(i, nb - 1 - n).start()
        return c

    lax.fori_loop(0, nb, load, 0)

    barrier = pltpu.get_barrier_semaphore()
    peers = [r * 2 + core for r in rel] + [sib]
    for p in peers:
        pl.semaphore_signal(barrier, inc=1, device_id={'cp': p}, device_id_type=MESH)
    lse_copy.wait()

    eye = (lax.broadcasted_iota(jnp.int32, (ROWS, ROWS), 0)
           == lax.broadcasted_iota(jnp.int32, (ROWS, ROWS), 1))

    def prepare(b):
        for i in range(5):
            raw_copy(i, b).wait()
        for i in range(4):
            xs[b, :, i] = jnp.swapaxes(raw[b, i], 0, 1)
        oh = jnp.swapaxes(raw[b, 4], 0, 1)
        lse = lsev[:, rows(b)] * LOG2E
        for h in range(4):
            g = _dot(xs[b, h, 1], oh[h], 1, 1)
            auxs[b, h, 0] = lse[h:h + 1]
            auxs[b, h, 1] = jnp.sum(jnp.where(eye, g, 0.0), axis=0, keepdims=True)

    def dispatch(b):
        for d in (2, 0, 1):
            aux_send(b, d).start()
            in_send(b, d).start()
        rx[b, chip] = xs[b, chip]
        axr[b, core, chip] = auxs[b, chip]

    prepare(nb - 1)
    pl.semaphore_wait(barrier, 4)
    dispatch(nb - 1)

    def issue(n, c):
        b = nb - 1 - n
        prepare(b)
        dispatch(b)
        return c

    lax.fori_loop(1, nb, issue, 0)

    kidx = lax.broadcasted_iota(jnp.int32, (tile, 1), 0)
    qidx = lax.broadcasted_iota(jnp.int32, (1, tile), 1)
    kpos = (kidx % ROWS) * 8 + (kidx // ROWS) * 2 + core

    def pair(b, qb, other, diag, fresh=False):
        if other:
            q = rs[qb, :, 0].reshape(tile, hd)
            do = rs[qb, :, 1].reshape(tile, hd)
            par = 1 - core
        else:
            q = rx[qb, :, 0].reshape(tile, hd)
            do = rx[qb, :, 1].reshape(tile, hd)
            par = core
        k = rx[b, :, 2].reshape(tile, hd)
        v = rx[b, :, 3].reshape(tile, hd)
        lse = jnp.concatenate([axr[qb, par, i, 0] for i in range(4)], axis=1)
        dd = jnp.concatenate([axr[qb, par, i, 1] for i in range(4)], axis=1)
        s = _dot(k, q, 1, 1)
        p = jnp.exp2(s * (scale * LOG2E) - lse)
        if diag:
            qpos = (qidx % ROWS) * 8 + (qidx // ROWS) * 2 + par
            p = jnp.where(kpos <= qpos, p, 0.0)
        dp = _dot(v, do, 1, 1)
        ds = (p * (dp - dd)).astype(BF16)
        gv = _dot(p.astype(BF16), do, 1, 0)
        gk = _dot(ds, q, 1, 0)
        gq = _dot(kt[...], ds, 1, 0)
        if fresh:
            dv[...] = gv
            dk[...] = gk
        else:
            dv[...] += gv
            dk[...] += gk
        if diag:
            dqt[int(other), qb] = gq
        else:
            dqt[int(other), qb] += gq

    def arrive(b):
        for d in range(3):
            in_recv(b, d).wait_recv()
            aux_recv(b, d).wait_recv()
        forward(b).start()
        aux_forward(b).start()
        kt[...] = rx[b, :, 2].reshape(tile, hd).astype(F32).T.astype(BF16)

    def emit_kv(b):
        okv[b, 0] = (dk[...] * scale).astype(BF16).reshape(4, ROWS, hd)
        okv[b, 1] = dv[...].astype(BF16).reshape(4, ROWS, hd)
        for d in (2, 0, 1):
            kv_send(b, d).start()
        orx[b, 1:3, chip] = okv[b, :, chip]

    def step(n, c):
        b = nb - 1 - n
        arrive(b)
        pair(b, b, False, True, fresh=True)

        def own(i, c):
            pair(b, i, False, False)
            return c

        lax.fori_loop(b + 1, nb, own, 0)
        forward(b).wait_recv()
        aux_forwarded(b).wait_recv()
        pair(b, b, True, True)

        def oth(i, c):
            pair(b, i, True, False)
            return c

        lax.fori_loop(b + 1, nb, oth, 0)
        emit_kv(b)
        return c

    lax.fori_loop(0, nb - 1, step, 0)

    arrive(0)
    dv[...] = jnp.zeros_like(dv)
    dk[...] = jnp.zeros_like(dk)

    def finish(i):
        part_send(i).wait_recv()
        g = (dqt[0, i] + dqp[i]) * scale
        oq[i] = g.T.astype(BF16).reshape(4, ROWS, hd)
        for d in (2, 0, 1):
            q_send(i, d).start()
        orx[i, 0, chip] = oq[i, chip]

    def last_oth(n, c):
        i = nb - 1 - n
        pair(0, i, True, False)
        part_send(i).start()
        return c

    lax.fori_loop(0, nb - 1, last_oth, 0)
    forward(0).wait_recv()
    aux_forwarded(0).wait_recv()
    pair(0, 0, True, True)
    part_send(0).start()

    def last_own(n, c):
        i = nb - 1 - n
        pair(0, i, False, False)
        finish(i)
        return c

    lax.fori_loop(0, nb - 1, last_own, 0)
    pair(0, 0, False, True)
    emit_kv(0)
    finish(0)

    def put(a, b):
        ost[b, a] = jnp.swapaxes(orx[b, a], 0, 1)
        out_copy(a, b).start()

    def out_kv(b):
        for d in range(3):
            kv_recv(b, d).wait_recv()
        put(1, b)
        put(2, b)

    def out_q(b):
        for d in range(3):
            q_recv(b, d).wait_recv()
        put(0, b)

    def drain_kv(n, c):
        out_kv(nb - 1 - n)
        return c

    def drain_q(n, c):
        out_q(nb - 1 - n)
        return c

    lax.fori_loop(0, nb - 1, drain_kv, 0)
    lax.fori_loop(0, nb - 1, drain_q, 0)
    out_kv(0)
    out_q(0)

    def drain(b, c):
        for d in range(3):
            in_send(b, d).wait_send()
            aux_send(b, d).wait_send()
            kv_send(b, d).wait_send()
            q_send(b, d).wait_send()
        forward(b).wait_send()
        aux_forward(b).wait_send()
        part_send(b).wait_send()
        for a in range(3):
            out_copy(a, b).wait()
        return c

    lax.fori_loop(0, nb, drain, 0)


def solution(mesh):
    rows = P(('data', 'cp'))
    cols = P(None, ('data', 'cp'))

    def local(q, k, v, o, dout, lse):
        c, h, d = q.shape
        nb = c // ROWS
        vm, dma = pltpu.VMEM, pltpu.SemaphoreType.DMA
        any_ = pl.BlockSpec(memory_space=pl.ANY)
        return pl.pallas_call(
            functools.partial(_kernel, nb),
            out_shape=[jax.ShapeDtypeStruct((c, h, d), BF16)] * 3,
            in_specs=[any_] * 6,
            out_specs=[any_] * 3,
            scratch_shapes=[
                vm((nb, 5, ROWS, h, d), BF16),
                vm((h, c), F32),
                vm((nb, h, 4, ROWS, d), BF16),
                vm((nb, h, 2, 1, ROWS), F32),
                vm((nb, 4, 4, ROWS, d), BF16),
                vm((nb, 4, 2, ROWS, d), BF16),
                vm((nb, 2, 4, 2, 1, ROWS), F32),
                vm((d, 4 * ROWS), BF16),
                vm((4 * ROWS, d), F32),
                vm((4 * ROWS, d), F32),
                vm((2, nb, d, 4 * ROWS), F32),
                vm((nb, d, 4 * ROWS), F32),
                vm((nb, 2, 4, ROWS, d), BF16),
                vm((nb, 4, ROWS, d), BF16),
                vm((nb, 3, h, ROWS, d), BF16),
                vm((nb, 3, ROWS, h, d), BF16),
                dma((nb, 5)), dma((1,)),
                dma((nb, 3)), dma((nb, 3)),
                dma((nb,)), dma((nb,)),
                dma((nb, 3)), dma((nb, 3)),
                dma((nb,)), dma((nb,)),
                dma((nb, 3)), dma((nb, 3)),
                dma((nb,)), dma((nb,)),
                dma((nb, 3)), dma((nb, 3)),
                dma((nb, 3)),
            ],
            compiler_params=pltpu.CompilerParams(
                collective_id=0, has_side_effects=True, vmem_limit_bytes=VMEM_LIMIT),
            name='attn_bwd',
        )(q, dout, k, v, o, lse)

    return jax.shard_map(local, mesh=mesh, in_specs=(rows, rows, rows, rows, rows, cols),
                         out_specs=(rows, rows, rows), check_vma=False)
```

time: 106 us -> 97.7 us (0.922)
  local copies, waits for them, and re-layouts: 10.1 us -> 4.88 us
  other arithmetic: 4.13 us -> 0 us
    another operation x2 -> x0, local copies, waits for them, and re-layouts: 2.23 us -> none  [local(): x = jnp.stack([a.transpose(1, 0, 2) for a in (q, dout, k, v)])]
    another operation x1 -> x0, other arithmetic: 2.22 us -> none  [local(): x = jnp.stack([a.transpose(1, 0, 2) for a in (q, dout, k, v)])]
    transpose x1 -> x0, local copies, waits for them, and re-layouts: 2.06 us -> none  [local(): return tuple((out[i].transpose(1, 0, 2) for i in range(3)))]
    unnamed x1 -> x0, other arithmetic: 1.25 us -> none
    unnamed x11 -> x9, local copies, waits for them, and re-layouts: 5.54 us -> 4.88 us
where the time goes in v2:
time: 97.7 us; the launch traced here: 97.4 us
  Pallas kernels  91.9 us (94%)
  local copies, waits for them, and re-layouts  4.88 us (5%)
    pallas_call x1, Pallas kernels, local(): pl.pallas_call(functools.partial(_kernel, nb), out_shape=[jax.ShapeDtypeS...  91.9 us
    unnamed x9, local copies, waits for them, and re-layouts  4.88 us

profile of v2, /device:TPU:0, one launch (start us, length us, event | category | flops | bytes accessed | tf_op | source)
XLA Modules:
  0.0 97.4 jit_solution(2532334036639653457)
XLA Ops:
  0.6 0.0 copy-start
  0.6 0.7 copy-done
  1.4 91.9 %attn_bwd.1 = (bf16[1024,4,128]{2,1,0:T(4,128)(2,1)S(1)}, bf16[1024,4,128]{2,1,0:T(4,128)(2,1)}, bf16[1024,4,128]{2,1,0:T(4,128)(2,1)}) custom-call(bf16[1024,4,128]{2,1,0:T(4,128)(2,1)} %q_in.1, bf16[1024,4,128]{2,1,0:T(4,128)(2,1)} %do_in.1, bf16[1024,4,128]{2,1,0:T(4,128)(2,1)} %k_in.1, bf16[1024,4,128]{2,1,0:T(4,128)(2,1)} %v_in.1, ...), custom_call_target="tpu_custom_call" | custom-call | tf_op jit(solution)/shard_map/attn_bwd/pallas_call | solution.py:302
  93.2 0.0 copy-start.2
  93.3 1.0 copy.12
  94.2 0.6 copy-done.2
  94.9 0.0 copy-start.1
  94.9 1.0 copy.13
  95.8 0.6 copy-done.1
  96.5 1.0 copy.14
Async XLA Ops:
  0.6 0.7 copy-start
  93.2 1.6 %copy-start.2 = (bf16[1024,4,128]{2,1,0:T(4,128)(2,1)S(1)}, bf16[1024,4,128]{2,1,0:T(4,128)(2,1)}, u32[]{:S(2)}) copy-start(bf16[1024,4,128]{2,1,0:T(4,128)(2,1)} %get-tuple-element.7) | copy-start | bytes 3145732
  94.9 1.6 %copy-start.1 = (bf16[1024,4,128]{2,1,0:T(4,128)(2,1)S(1)}, bf16[1024,4,128]{2,1,0:T(4,128)(2,1)}, u32[]{:S(2)}) copy-start(bf16[1024,4,128]{2,1,0:T(4,128)(2,1)} %get-tuple-element.8) | copy-start | bytes 3145732

commit v3 on v2

--- a/solution.py
+++ b/solution.py
@@ -12,7 +12,7 @@
 F32 = jnp.float32
 BF16 = jnp.bfloat16
 ROWS = 128
-VMEM_LIMIT = 52 << 20
+VMEM_LIMIT = 50 << 20
 LOG2E = math.log2(math.e)
 
 
@@ -21,9 +21,9 @@
 
 
 def _kernel(nb, q_in, do_in, k_in, v_in, o_in, lse_in, dq_out, dk_out, dv_out,
-            raw, lsev, xs, auxs, rx, rs, axr, kt, dk, dv, dqt, dqp, okv, oq, orx, ost,
+            raw, lsev, xs, auxs, rx, rs, axr, kt, dk, dv, dqt, dqp, okv, oq, orx,
             raw_l, lse_l, in_s, in_r, fw_s, fw_r, ax_s, ax_r, fa_s, fa_r, kv_s, kv_r,
-            qp_s, qp_r, oq_s, oq_r, out_l):
+            qp_s, qp_r, oq_s, oq_r):
     hd = q_in.shape[-1]
     tile = 4 * ROWS
     scale = hd ** -0.5
@@ -80,9 +80,6 @@
 
     def q_recv(b, d):
         return remote(oq.at[b, rel[d]], orx.at[b, 0, rel[d]], oq_s.at[b, d], oq_r.at[b, d], rel[d] * 2 + core)
-
-    def out_copy(a, b):
-        return pltpu.make_async_copy(ost.at[b, a], (dq_out, dk_out, dv_out)[a].at[rows(b)], out_l.at[b, a])
 
     lse_copy = pltpu.make_async_copy(lse_in, lsev, lse_l.at[0])
     lse_copy.start()
@@ -178,7 +175,15 @@
             aux_recv(b, d).wait_recv()
         forward(b).start()
         aux_forward(b).start()
+
+    def both(b, qb, diag):
+        pair(b, qb, False, diag, fresh=diag)
+        pair(b, qb, True, diag)
+
+    def begin(b):
         kt[...] = rx[b, :, 2].reshape(tile, hd).astype(F32).T.astype(BF16)
+        forward(b).wait_recv()
+        aux_forwarded(b).wait_recv()
 
     def emit_kv(b):
         okv[b, 0] = (dk[...] * scale).astype(BF16).reshape(4, ROWS, hd)
@@ -189,31 +194,27 @@
 
     def step(n, c):
         b = nb - 1 - n
-        arrive(b)
-        pair(b, b, False, True, fresh=True)
-
-        def own(i, c):
-            pair(b, i, False, False)
+        begin(b)
+        both(b, b, True)
+
+        @pl.when(n == 0)
+        def _():
+            arrive(b - 1)
+
+        def off(i, c):
+            @pl.when(i == nb - 1)
+            def _():
+                arrive(b - 1)
+
+            both(b, i, False)
             return c
 
-        lax.fori_loop(b + 1, nb, own, 0)
-        forward(b).wait_recv()
-        aux_forwarded(b).wait_recv()
-        pair(b, b, True, True)
-
-        def oth(i, c):
-            pair(b, i, True, False)
-            return c
-
-        lax.fori_loop(b + 1, nb, oth, 0)
+        lax.fori_loop(b + 1, nb, off, 0)
         emit_kv(b)
         return c
 
+    arrive(nb - 1)
     lax.fori_loop(0, nb - 1, step, 0)
-
-    arrive(0)
-    dv[...] = jnp.zeros_like(dv)
-    dk[...] = jnp.zeros_like(dk)
 
     def finish(i):
         part_send(i).wait_recv()
@@ -223,32 +224,31 @@
             q_send(i, d).start()
         orx[i, 0, chip] = oq[i, chip]
 
-    def last_oth(n, c):
+    begin(0)
+    dv[...] = jnp.zeros_like(dv)
+    dk[...] = jnp.zeros_like(dk)
+
+    def last(n, c):
         i = nb - 1 - n
-        pair(0, i, True, False)
+        both(0, i, False)
         part_send(i).start()
-        return c
-
-    lax.fori_loop(0, nb - 1, last_oth, 0)
-    forward(0).wait_recv()
-    aux_forwarded(0).wait_recv()
+
+        @pl.when(n > 0)
+        def _():
+            finish(i + 1)
+
+        return c
+
+    lax.fori_loop(0, nb - 1, last, 0)
     pair(0, 0, True, True)
     part_send(0).start()
-
-    def last_own(n, c):
-        i = nb - 1 - n
-        pair(0, i, False, False)
-        finish(i)
-        return c
-
-    lax.fori_loop(0, nb - 1, last_own, 0)
     pair(0, 0, False, True)
     emit_kv(0)
+    finish(1)
     finish(0)
 
     def put(a, b):
-        ost[b, a] = jnp.swapaxes(orx[b, a], 0, 1)
-        out_copy(a, b).start()
+        (dq_out, dk_out, dv_out)[a][rows(b)] = jnp.swapaxes(orx[b, a], 0, 1)
 
     def out_kv(b):
         for d in range(3):
@@ -283,11 +283,17 @@
         forward(b).wait_send()
         aux_forward(b).wait_send()
         part_send(b).wait_send()
-        for a in range(3):
-            out_copy(a, b).wait()
         return c
 
     lax.fori_loop(0, nb, drain, 0)
+
+
+def _store(a, b, c, x, y, z, sem):
+    copies = [pltpu.make_async_copy(s, t, sem.at[i]) for i, (s, t) in enumerate(((a, x), (b, y), (c, z)))]
+    for copy in copies:
+        copy.start()
+    for copy in copies:
+        copy.wait()
 
 
 def solution(mesh):
@@ -298,12 +304,12 @@
         c, h, d = q.shape
         nb = c // ROWS
         vm, dma = pltpu.VMEM, pltpu.SemaphoreType.DMA
-        any_ = pl.BlockSpec(memory_space=pl.ANY)
-        return pl.pallas_call(
+        hbm = pl.BlockSpec(memory_space=pl.ANY)
+        grads = pl.pallas_call(
             functools.partial(_kernel, nb),
             out_shape=[jax.ShapeDtypeStruct((c, h, d), BF16)] * 3,
-            in_specs=[any_] * 6,
-            out_specs=[any_] * 3,
+            in_specs=[hbm] * 6,
+            out_specs=[pl.BlockSpec(memory_space=pltpu.VMEM)] * 3,
             scratch_shapes=[
                 vm((nb, 5, ROWS, h, d), BF16),
                 vm((h, c), F32),
@@ -320,7 +326,6 @@
                 vm((nb, 2, 4, ROWS, d), BF16),
                 vm((nb, 4, ROWS, d), BF16),
                 vm((nb, 3, h, ROWS, d), BF16),
-                vm((nb, 3, ROWS, h, d), BF16),
                 dma((nb, 5)), dma((1,)),
                 dma((nb, 3)), dma((nb, 3)),
                 dma((nb,)), dma((nb,)),
@@ -329,12 +334,20 @@
                 dma((nb, 3)), dma((nb, 3)),
                 dma((nb,)), dma((nb,)),
                 dma((nb, 3)), dma((nb, 3)),
-                dma((nb, 3)),
             ],
             compiler_params=pltpu.CompilerParams(
                 collective_id=0, has_side_effects=True, vmem_limit_bytes=VMEM_LIMIT),
             name='attn_bwd',
         )(q, dout, k, v, o, lse)
+        return pl.pallas_call(
+            _store,
+            out_shape=[jax.ShapeDtypeStruct((c, h, d), BF16)] * 3,
+            in_specs=[pl.BlockSpec(memory_space=pltpu.VMEM)] * 3,
+            out_specs=[hbm] * 3,
+            scratch_shapes=[dma((3,))],
+            compiler_params=pltpu.CompilerParams(vmem_limit_bytes=8 << 20),
+            name='store',
+        )(*grads)
 
     return jax.shard_map(local, mesh=mesh, in_specs=(rows, rows, rows, rows, rows, cols),
                          out_specs=(rows, rows, rows), check_vma=False)

time: 97.7 us -> 91.2 us (0.933)
  local copies, waits for them, and re-layouts: 4.88 us -> 0.71 us
  Pallas kernels: 91.9 us -> 89.6 us
    unnamed x9 -> x2, local copies, waits for them, and re-layouts: 4.88 us -> 0.71 us
    pallas_call x1, Pallas kernels: 91.9 us -> 87.9 us  [local(): pl.pallas_call(functools.partial(_kernel, nb), out_shape=[jax.ShapeDtypeS...]
    pallas_call x0 -> x1, Pallas kernels: none -> 1.69 us  [local(): pl.pallas_call(_store, out_shape=[jax.ShapeDtypeStruct((c, h, d), BF16)]...]
where the time goes in v3:
time: 91.2 us; the launch traced here: 91 us
  Pallas kernels  89.6 us (98%)
    pallas_call x1, Pallas kernels, local(): pl.pallas_call(functools.partial(_kernel, nb), out_shape=[jax.ShapeDtypeS...  87.9 us

profile of v3, /device:TPU:0, one launch (start us, length us, event | category | flops | bytes accessed | tf_op | source)
XLA Modules:
  0.0 91.0 jit_solution(1862221513156892423)
XLA Ops:
  0.6 0.0 copy-start
  0.6 0.7 copy-done
  1.4 87.9 %attn_bwd.1 = (bf16[1024,4,128]{2,1,0:T(4,128)(2,1)S(1)}, bf16[1024,4,128]{2,1,0:T(4,128)(2,1)S(1)}, bf16[1024,4,128]{2,1,0:T(4,128)(2,1)S(1)}) custom-call(bf16[1024,4,128]{2,1,0:T(4,128)(2,1)} %q_in.1, bf16[1024,4,128]{2,1,0:T(4,128)(2,1)} %do_in.1, bf16[1024,4,128]{2,1,0:T(4,128)(2,1)} %k_in.1, bf16[1024,4,128]{2,1,0:T(4,128)(2,1)} %v_in.1, ...), custom_call_target="tpu_custom_call" | custom-call | tf_op jit(solution)/shard_map/attn_bwd/pallas_call | solution.py:308
  89.3 1.7 %store.1 = (bf16[1024,4,128]{2,1,0:T(4,128)(2,1)}, bf16[1024,4,128]{2,1,0:T(4,128)(2,1)}, bf16[1024,4,128]{2,1,0:T(4,128)(2,1)}) custom-call(bf16[1024,4,128]{2,1,0:T(4,128)(2,1)S(1)} %get-tuple-element.6.a, bf16[1024,4,128]{2,1,0:T(4,128)(2,1)S(1)} %get-tuple-element.7.b, bf16[1024,4,128]{2,1,0:T(4,128)(2,1)S(1)} %get-tuple-element.8.c), custom_call_target="tpu_custom_call" | custom-call | tf_op jit(solution)/shard_map/store/pallas_call | solution.py:342
Async XLA Ops:
  0.6 0.7 copy-start

commit v4 on v3

--- a/solution.py
+++ b/solution.py
@@ -81,52 +81,58 @@
     def q_recv(b, d):
         return remote(oq.at[b, rel[d]], orx.at[b, 0, rel[d]], oq_s.at[b, d], oq_r.at[b, d], rel[d] * 2 + core)
 
-    lse_copy = pltpu.make_async_copy(lse_in, lsev, lse_l.at[0])
-    lse_copy.start()
-
-    def load(n, c):
-        for i in range(5):
-            raw_copy(i, nb - 1 - n).start()
-        return c
-
-    lax.fori_loop(0, nb, load, 0)
-
     barrier = pltpu.get_barrier_semaphore()
     peers = [r * 2 + core for r in rel] + [sib]
     for p in peers:
         pl.semaphore_signal(barrier, inc=1, device_id={'cp': p}, device_id_type=MESH)
-    lse_copy.wait()
+
+    for i in range(5):
+        raw_copy(i, nb - 1).start()
+    lse_copy = pltpu.make_async_copy(lse_in, lsev, lse_l.at[0])
+    lse_copy.start()
 
     eye = (lax.broadcasted_iota(jnp.int32, (ROWS, ROWS), 0)
            == lax.broadcasted_iota(jnp.int32, (ROWS, ROWS), 1))
 
-    def prepare(b):
-        for i in range(5):
+    def relayout(b):
+        for i in range(4):
             raw_copy(i, b).wait()
-        for i in range(4):
             xs[b, :, i] = jnp.swapaxes(raw[b, i], 0, 1)
+
+    def dispatch(b):
+        for d in (2, 0, 1):
+            in_send(b, d).start()
+
+    def stats(b):
+        raw_copy(4, b).wait()
         oh = jnp.swapaxes(raw[b, 4], 0, 1)
         lse = lsev[:, rows(b)] * LOG2E
         for h in range(4):
             g = _dot(xs[b, h, 1], oh[h], 1, 1)
             auxs[b, h, 0] = lse[h:h + 1]
             auxs[b, h, 1] = jnp.sum(jnp.where(eye, g, 0.0), axis=0, keepdims=True)
-
-    def dispatch(b):
         for d in (2, 0, 1):
             aux_send(b, d).start()
-            in_send(b, d).start()
         rx[b, chip] = xs[b, chip]
         axr[b, core, chip] = auxs[b, chip]
 
-    prepare(nb - 1)
+    def load(n, c):
+        for i in range(5):
+            raw_copy(i, nb - 1 - n).start()
+        return c
+
+    relayout(nb - 1)
     pl.semaphore_wait(barrier, 4)
     dispatch(nb - 1)
+    lax.fori_loop(1, nb, load, 0)
+    lse_copy.wait()
+    stats(nb - 1)
 
     def issue(n, c):
         b = nb - 1 - n
-        prepare(b)
+        relayout(b)
         dispatch(b)
+        stats(b)
         return c
 
     lax.fori_loop(1, nb, issue, 0)

time: 91.2 us -> 90.7 us (level)
  no operation moved by 1% of the time
where the time goes in v4:
time: 90.7 us; the launch traced here: 90.5 us
  Pallas kernels  89.1 us (98%)
    pallas_call x1, Pallas kernels, local(): pl.pallas_call(functools.partial(_kernel, nb), out_shape=[jax.ShapeDtypeS...  87.4 us

profile of v4, /device:TPU:0, one launch (start us, length us, event | category | flops | bytes accessed | tf_op | source)
XLA Modules:
  0.0 90.5 jit_solution(1237804253418282837)
XLA Ops:
  0.6 0.0 copy-start
  0.6 0.7 copy-done
  1.4 87.4 %attn_bwd.1 = (bf16[1024,4,128]{2,1,0:T(4,128)(2,1)S(1)}, bf16[1024,4,128]{2,1,0:T(4,128)(2,1)S(1)}, bf16[1024,4,128]{2,1,0:T(4,128)(2,1)S(1)}) custom-call(bf16[1024,4,128]{2,1,0:T(4,128)(2,1)} %q_in.1, bf16[1024,4,128]{2,1,0:T(4,128)(2,1)} %do_in.1, bf16[1024,4,128]{2,1,0:T(4,128)(2,1)} %k_in.1, bf16[1024,4,128]{2,1,0:T(4,128)(2,1)} %v_in.1, ...), custom_call_target="tpu_custom_call" | custom-call | tf_op jit(solution)/shard_map/attn_bwd/pallas_call | solution.py:314
  88.8 1.7 %store.1 = (bf16[1024,4,128]{2,1,0:T(4,128)(2,1)}, bf16[1024,4,128]{2,1,0:T(4,128)(2,1)}, bf16[1024,4,128]{2,1,0:T(4,128)(2,1)}) custom-call(bf16[1024,4,128]{2,1,0:T(4,128)(2,1)S(1)} %get-tuple-element.6.a, bf16[1024,4,128]{2,1,0:T(4,128)(2,1)S(1)} %get-tuple-element.7.b, bf16[1024,4,128]{2,1,0:T(4,128)(2,1)S(1)} %get-tuple-element.8.c), custom_call_target="tpu_custom_call" | custom-call | tf_op jit(solution)/shard_map/store/pallas_call | solution.py:348
Async XLA Ops:
  0.6 0.7 copy-start

commit v5 on v4

--- a/solution.py
+++ b/solution.py
@@ -43,51 +43,46 @@
 
     def raw_copy(i, b):
         src = (q_in, do_in, k_in, v_in, o_in)[i]
-        return pltpu.make_async_copy(src.at[rows(b)], raw.at[b, i], raw_l.at[b, i])
+        return pltpu.make_async_copy(src.at[rows(b)], raw.at[b, i], raw_l.at[b % 2])
+
+    def landed(ref, sem):
+        pltpu.make_async_copy(ref, ref, sem).wait()
 
     def in_send(b, d):
-        return remote(xs.at[b, rel[d]], rx.at[b, chip], in_s.at[b, d], in_r.at[b, d], rel[d] * 2 + core)
-
-    def in_recv(b, d):
-        return remote(xs.at[b, rel[d]], rx.at[b, rel[d]], in_s.at[b, d], in_r.at[b, d], rel[d] * 2 + core)
+        return remote(xs.at[b, rel[d]], rx.at[b, chip], in_s.at[0], in_r.at[b], rel[d] * 2 + core)
 
     def aux_send(b, d):
-        return remote(auxs.at[b, rel[d]], axr.at[b, core, chip], ax_s.at[b, d], ax_r.at[b, d], rel[d] * 2 + core)
-
-    def aux_recv(b, d):
-        return remote(auxs.at[b, rel[d]], axr.at[b, core, rel[d]], ax_s.at[b, d], ax_r.at[b, d], rel[d] * 2 + core)
+        return remote(auxs.at[b, rel[d]], axr.at[b, core, chip], ax_s.at[0], ax_r.at[b], rel[d] * 2 + core)
 
     def forward(b):
-        return remote(rx.at[b, :, 0:2], rs.at[b], fw_s.at[b], fw_r.at[b], sib)
+        return remote(rx.at[b, :, 0:2], rs.at[b], fw_s.at[0], fw_r.at[b % 2], sib)
 
     def aux_forward(b):
-        return remote(axr.at[b, core], axr.at[b, core], fa_s.at[b], fa_r.at[b], sib)
+        return remote(axr.at[b, core], axr.at[b, core], fa_s.at[0], fa_r.at[b % 2], sib)
 
     def aux_forwarded(b):
-        return remote(axr.at[b, core], axr.at[b, 1 - core], fa_s.at[b], fa_r.at[b], sib)
-
-    def kv_send(b, d):
-        return remote(okv.at[b, :, rel[d]], orx.at[b, 1:3, chip], kv_s.at[b, d], kv_r.at[b, d], rel[d] * 2 + core)
-
-    def kv_recv(b, d):
-        return remote(okv.at[b, :, rel[d]], orx.at[b, 1:3, rel[d]], kv_s.at[b, d], kv_r.at[b, d], rel[d] * 2 + core)
+        return remote(axr.at[b, core], axr.at[b, 1 - core], fa_s.at[0], fa_r.at[b % 2], sib)
+
+    def kv_send(b, d, g):
+        return remote(okv.at[b, :, rel[d]], orx.at[b, 1:3, chip], kv_s.at[0], kv_r.at[g], rel[d] * 2 + core)
 
     def part_send(b):
-        return remote(dqt.at[1, b], dqp.at[b], qp_s.at[b], qp_r.at[b], sib)
-
-    def q_send(b, d):
-        return remote(oq.at[b, rel[d]], orx.at[b, 0, chip], oq_s.at[b, d], oq_r.at[b, d], rel[d] * 2 + core)
-
-    def q_recv(b, d):
-        return remote(oq.at[b, rel[d]], orx.at[b, 0, rel[d]], oq_s.at[b, d], oq_r.at[b, d], rel[d] * 2 + core)
+        return remote(dqt.at[1, b], dqp.at[b], qp_s.at[0], qp_r.at[b], sib)
+
+    def q_send(b, d, g):
+        return remote(oq.at[b, rel[d]], orx.at[b, 0, chip], oq_s.at[0], oq_r.at[g], rel[d] * 2 + core)
 
     barrier = pltpu.get_barrier_semaphore()
     peers = [r * 2 + core for r in rel] + [sib]
     for p in peers:
         pl.semaphore_signal(barrier, inc=1, device_id={'cp': p}, device_id_type=MESH)
 
-    for i in range(5):
-        raw_copy(i, nb - 1).start()
+    def load(b):
+        for i in range(5):
+            raw_copy(i, b).start()
+
+    load(nb - 1)
+    load(nb - 2)
     lse_copy = pltpu.make_async_copy(lse_in, lsev, lse_l.at[0])
     lse_copy.start()
 
@@ -95,8 +90,8 @@
            == lax.broadcasted_iota(jnp.int32, (ROWS, ROWS), 1))
 
     def relayout(b):
+        landed(raw.at[b], raw_l.at[b % 2])
         for i in range(4):
-            raw_copy(i, b).wait()
             xs[b, :, i] = jnp.swapaxes(raw[b, i], 0, 1)
 
     def dispatch(b):
@@ -104,7 +99,6 @@
             in_send(b, d).start()
 
     def stats(b):
-        raw_copy(4, b).wait()
         oh = jnp.swapaxes(raw[b, 4], 0, 1)
         lse = lsev[:, rows(b)] * LOG2E
         for h in range(4):
@@ -116,15 +110,10 @@
         rx[b, chip] = xs[b, chip]
         axr[b, core, chip] = auxs[b, chip]
 
-    def load(n, c):
-        for i in range(5):
-            raw_copy(i, nb - 1 - n).start()
-        return c
-
     relayout(nb - 1)
     pl.semaphore_wait(barrier, 4)
     dispatch(nb - 1)
-    lax.fori_loop(1, nb, load, 0)
+    load(nb - 3)
     lse_copy.wait()
     stats(nb - 1)
 
@@ -132,6 +121,11 @@
         b = nb - 1 - n
         relayout(b)
         dispatch(b)
+
+        @pl.when(b >= 2)
+        def _():
+            load(b - 2)
+
         stats(b)
         return c
 
@@ -176,9 +170,8 @@
             dqt[int(other), qb] += gq
 
     def arrive(b):
-        for d in range(3):
-            in_recv(b, d).wait_recv()
-            aux_recv(b, d).wait_recv()
+        landed(rx.at[b, 0:3], in_r.at[b])
+        landed(axr.at[b, 0, 0:3], ax_r.at[b])
         forward(b).start()
         aux_forward(b).start()
 
@@ -191,11 +184,11 @@
         forward(b).wait_recv()
         aux_forwarded(b).wait_recv()
 
-    def emit_kv(b):
+    def emit_kv(b, g):
         okv[b, 0] = (dk[...] * scale).astype(BF16).reshape(4, ROWS, hd)
         okv[b, 1] = dv[...].astype(BF16).reshape(4, ROWS, hd)
         for d in (2, 0, 1):
-            kv_send(b, d).start()
+            kv_send(b, d, g).start()
         orx[b, 1:3, chip] = okv[b, :, chip]
 
     def step(n, c):
@@ -216,18 +209,18 @@
             return c
 
         lax.fori_loop(b + 1, nb, off, 0)
-        emit_kv(b)
+        emit_kv(b, n // (nb - 2))
         return c
 
     arrive(nb - 1)
     lax.fori_loop(0, nb - 1, step, 0)
 
-    def finish(i):
+    def finish(i, g):
         part_send(i).wait_recv()
-        g = (dqt[0, i] + dqp[i]) * scale
-        oq[i] = g.T.astype(BF16).reshape(4, ROWS, hd)
+        total = (dqt[0, i] + dqp[i]) * scale
+        oq[i] = total.T.astype(BF16).reshape(4, ROWS, hd)
         for d in (2, 0, 1):
-            q_send(i, d).start()
+            q_send(i, d, g).start()
         orx[i, 0, chip] = oq[i, chip]
 
     begin(0)
@@ -241,7 +234,7 @@
 
         @pl.when(n > 0)
         def _():
-            finish(i + 1)
+            finish(i + 1, (nb - 2 - i) // 4)
 
         return c
 
@@ -249,49 +242,46 @@
     pair(0, 0, True, True)
     part_send(0).start()
     pair(0, 0, False, True)
-    emit_kv(0)
-    finish(1)
-    finish(0)
+    emit_kv(0, 2)
+    finish(1, 2)
+    finish(0, 3)
 
     def put(a, b):
         (dq_out, dk_out, dv_out)[a][rows(b)] = jnp.swapaxes(orx[b, a], 0, 1)
 
-    def out_kv(b):
-        for d in range(3):
-            kv_recv(b, d).wait_recv()
+    def put_kv(b):
         put(1, b)
         put(2, b)
 
-    def out_q(b):
-        for d in range(3):
-            q_recv(b, d).wait_recv()
-        put(0, b)
-
-    def drain_kv(n, c):
-        out_kv(nb - 1 - n)
-        return c
-
-    def drain_q(n, c):
-        out_q(nb - 1 - n)
-        return c
-
-    lax.fori_loop(0, nb - 1, drain_kv, 0)
-    lax.fori_loop(0, nb - 1, drain_q, 0)
-    out_kv(0)
-    out_q(0)
-
-    def drain(b, c):
-        for d in range(3):
-            in_send(b, d).wait_send()
-            aux_send(b, d).wait_send()
-            kv_send(b, d).wait_send()
-            q_send(b, d).wait_send()
-        forward(b).wait_send()
-        aux_forward(b).wait_send()
-        part_send(b).wait_send()
-        return c
-
-    lax.fori_loop(0, nb, drain, 0)
+    def put_all(fn, lo, hi):
+        def body(n, c):
+            fn(hi - 1 - n)
+            return c
+
+        lax.fori_loop(0, hi - lo, body, 0)
+
+    landed(orx.at[2:nb, 1:3, 0:3], kv_r.at[0])
+    put_all(put_kv, 2, nb)
+    landed(orx.at[1, 1:3, 0:3], kv_r.at[1])
+    put_kv(1)
+    landed(orx.at[4:nb, 0, 0:3], oq_r.at[0])
+    put_all(functools.partial(put, 0), 4, nb)
+    landed(orx.at[2:4, 0, 0:3], oq_r.at[1])
+    put_all(functools.partial(put, 0), 2, 4)
+    landed(orx.at[0, 1:3, 0:3], kv_r.at[2])
+    put_kv(0)
+    landed(orx.at[1, 0, 0:3], oq_r.at[2])
+    put(0, 1)
+
+    landed(xs.at[:, 0:3], in_s.at[0])
+    landed(auxs.at[:, 0:3], ax_s.at[0])
+    landed(rx.at[:, :, 0:2], fw_s.at[0])
+    landed(axr.at[:, 0], fa_s.at[0])
+    landed(dqt.at[1], qp_s.at[0])
+    landed(okv.at[:, :, 0:3], kv_s.at[0])
+    landed(orx.at[0, 0, 0:3], oq_r.at[3])
+    put(0, 0)
+    landed(oq.at[:, 0:3], oq_s.at[0])
 
 
 def _store(a, b, c, x, y, z, sem):
@@ -332,19 +322,19 @@
                 vm((nb, 2, 4, ROWS, d), BF16),
                 vm((nb, 4, ROWS, d), BF16),
                 vm((nb, 3, h, ROWS, d), BF16),
-                dma((nb, 5)), dma((1,)),
-                dma((nb, 3)), dma((nb, 3)),
-                dma((nb,)), dma((nb,)),
-                dma((nb, 3)), dma((nb, 3)),
-                dma((nb,)), dma((nb,)),
-                dma((nb, 3)), dma((nb, 3)),
-                dma((nb,)), dma((nb,)),
-                dma((nb, 3)), dma((nb, 3)),
+                dma((2,)), dma((1,)),
+                dma((1,)), dma((nb,)),
+                dma((1,)), dma((2,)),
+                dma((1,)), dma((nb,)),
+                dma((1,)), dma((2,)),
+                dma((1,)), dma((3,)),
+                dma((1,)), dma((nb,)),
+                dma((1,)), dma((4,)),
             ],
             compiler_params=pltpu.CompilerParams(
                 collective_id=0, has_side_effects=True, vmem_limit_bytes=VMEM_LIMIT),
             name='attn_bwd',
-        )(q, dout, k, v, o, lse)
+        )(*(pltpu.with_memory_space_constraint(a, pltpu.HBM) for a in (q, dout, k, v, o, lse)))
         return pl.pallas_call(
             _store,
             out_shape=[jax.ShapeDtypeStruct((c, h, d), BF16)] * 3,

time: 90.7 us -> 88 us (0.970)
  Pallas kernels: 89.1 us -> 87.1 us
    pallas_call x1, Pallas kernels: 87.4 us -> 85.4 us  [local(): pl.pallas_call(functools.partial(_kernel, nb), out_shape=[jax.ShapeDtypeS...]
where the time goes in v5:
time: 88 us; the launch traced here: 87.8 us
  Pallas kernels  87.1 us (99%)
    pallas_call x1, Pallas kernels, local(): pl.pallas_call(functools.partial(_kernel, nb), out_shape=[jax.ShapeDtypeS...  85.4 us

profile of v5, /device:TPU:0, one launch (start us, length us, event | category | flops | bytes accessed | tf_op | source)
XLA Modules:
  0.0 87.8 jit_solution(5329252060152334844)
XLA Ops:
  0.6 85.4 %attn_bwd.1 = (bf16[1024,4,128]{2,1,0:T(4,128)(2,1)S(1)}, bf16[1024,4,128]{2,1,0:T(4,128)(2,1)S(1)}, bf16[1024,4,128]{2,1,0:T(4,128)(2,1)S(1)}) custom-call(bf16[1024,4,128]{2,1,0:T(4,128)(2,1)} %q_in.1, bf16[1024,4,128]{2,1,0:T(4,128)(2,1)} %do_in.1, bf16[1024,4,128]{2,1,0:T(4,128)(2,1)} %k_in.1, bf16[1024,4,128]{2,1,0:T(4,128)(2,1)} %v_in.1, ...), custom_call_target="tpu_custom_call" | custom-call | tf_op jit(solution)/shard_map/attn_bwd/pallas_call | solution.py:304
  86.1 1.7 %store.1 = (bf16[1024,4,128]{2,1,0:T(4,128)(2,1)}, bf16[1024,4,128]{2,1,0:T(4,128)(2,1)}, bf16[1024,4,128]{2,1,0:T(4,128)(2,1)}) custom-call(bf16[1024,4,128]{2,1,0:T(4,128)(2,1)S(1)} %get-tuple-element.6.a, bf16[1024,4,128]{2,1,0:T(4,128)(2,1)S(1)} %get-tuple-element.7.b, bf16[1024,4,128]{2,1,0:T(4,128)(2,1)S(1)} %get-tuple-element.8.c), custom_call_target="tpu_custom_call" | custom-call | tf_op jit(solution)/shard_map/store/pallas_call | solution.py:338

commit v6 on v5

--- a/solution.py
+++ b/solution.py
@@ -22,7 +22,7 @@
 
 def _kernel(nb, q_in, do_in, k_in, v_in, o_in, lse_in, dq_out, dk_out, dv_out,
             raw, lsev, xs, auxs, rx, rs, axr, kt, dk, dv, dqt, dqp, okv, oq, orx,
-            raw_l, lse_l, in_s, in_r, fw_s, fw_r, ax_s, ax_r, fa_s, fa_r, kv_s, kv_r,
+            raw_l, first_l, lse_l, in_s, in_r, fw_s, fw_r, ax_s, ax_r, fa_s, fa_r, kv_s, kv_r,
             qp_s, qp_r, oq_s, oq_r):
     hd = q_in.shape[-1]
     tile = 4 * ROWS
@@ -41,15 +41,18 @@
     def rows(b):
         return pl.ds(pl.multiple_of(b * ROWS, ROWS), ROWS)
 
-    def raw_copy(i, b):
+    def raw_copy(i, b, sem):
         src = (q_in, do_in, k_in, v_in, o_in)[i]
-        return pltpu.make_async_copy(src.at[rows(b)], raw.at[b, i], raw_l.at[b % 2])
+        return pltpu.make_async_copy(src.at[rows(b)], raw.at[b, i], sem)
 
     def landed(ref, sem):
         pltpu.make_async_copy(ref, ref, sem).wait()
 
     def in_send(b, d):
         return remote(xs.at[b, rel[d]], rx.at[b, chip], in_s.at[0], in_r.at[b], rel[d] * 2 + core)
+
+    def in_piece(b, d, i):
+        return remote(xs.at[b, rel[d], i], rx.at[b, chip, i], in_s.at[0], in_r.at[b], rel[d] * 2 + core)
 
     def aux_send(b, d):
         return remote(auxs.at[b, rel[d]], axr.at[b, core, chip], ax_s.at[0], ax_r.at[b], rel[d] * 2 + core)
@@ -79,10 +82,10 @@
 
     def load(b):
         for i in range(5):
-            raw_copy(i, b).start()
-
-    load(nb - 1)
-    load(nb - 2)
+            raw_copy(i, b, raw_l.at[b % 2]).start()
+
+    for i in range(5):
+        raw_copy(i, nb - 1, first_l.at[i]).start()
     lse_copy = pltpu.make_async_copy(lse_in, lsev, lse_l.at[0])
     lse_copy.start()
 
@@ -110,10 +113,17 @@
         rx[b, chip] = xs[b, chip]
         axr[b, core, chip] = auxs[b, chip]
 
-    relayout(nb - 1)
-    pl.semaphore_wait(barrier, 4)
-    dispatch(nb - 1)
+    last_block = nb - 1
+    for i in range(4):
+        raw_copy(i, last_block, first_l.at[i]).wait()
+        xs[last_block, :, i] = jnp.swapaxes(raw[last_block, i], 0, 1)
+        if i == 0:
+            pl.semaphore_wait(barrier, 4)
+        for d in (2, 0, 1):
+            in_piece(last_block, d, i).start()
+    load(nb - 2)
     load(nb - 3)
+    raw_copy(4, last_block, first_l.at[4]).wait()
     lse_copy.wait()
     stats(nb - 1)
 
@@ -322,7 +332,7 @@
                 vm((nb, 2, 4, ROWS, d), BF16),
                 vm((nb, 4, ROWS, d), BF16),
                 vm((nb, 3, h, ROWS, d), BF16),
-                dma((2,)), dma((1,)),
+                dma((2,)), dma((5,)), dma((1,)),
                 dma((1,)), dma((nb,)),
                 dma((1,)), dma((2,)),
                 dma((1,)), dma((nb,)),

time: 88 us -> 87.5 us (level)
  no operation moved by 1% of the time
where the time goes in v6:
time: 87.5 us; the launch traced here: 87.3 us
  Pallas kernels  86.6 us (99%)
    pallas_call x1, Pallas kernels, local(): pl.pallas_call(functools.partial(_kernel, nb), out_shape=[jax.ShapeDtypeS...  85 us

profile of v6, /device:TPU:0, one launch (start us, length us, event | category | flops | bytes accessed | tf_op | source)
XLA Modules:
  0.0 87.3 jit_solution(13057680247328561345)
XLA Ops:
  0.6 85.0 %attn_bwd.1 = (bf16[1024,4,128]{2,1,0:T(4,128)(2,1)S(1)}, bf16[1024,4,128]{2,1,0:T(4,128)(2,1)S(1)}, bf16[1024,4,128]{2,1,0:T(4,128)(2,1)S(1)}) custom-call(bf16[1024,4,128]{2,1,0:T(4,128)(2,1)} %q_in.1, bf16[1024,4,128]{2,1,0:T(4,128)(2,1)} %do_in.1, bf16[1024,4,128]{2,1,0:T(4,128)(2,1)} %k_in.1, bf16[1024,4,128]{2,1,0:T(4,128)(2,1)} %v_in.1, ...), custom_call_target="tpu_custom_call" | custom-call | tf_op jit(solution)/shard_map/attn_bwd/pallas_call | solution.py:314
  85.6 1.7 %store.1 = (bf16[1024,4,128]{2,1,0:T(4,128)(2,1)}, bf16[1024,4,128]{2,1,0:T(4,128)(2,1)}, bf16[1024,4,128]{2,1,0:T(4,128)(2,1)}) custom-call(bf16[1024,4,128]{2,1,0:T(4,128)(2,1)S(1)} %get-tuple-element.6.a, bf16[1024,4,128]{2,1,0:T(4,128)(2,1)S(1)} %get-tuple-element.7.b, bf16[1024,4,128]{2,1,0:T(4,128)(2,1)S(1)} %get-tuple-element.8.c), custom_call_target="tpu_custom_call" | custom-call | tf_op jit(solution)/shard_map/store/pallas_call | solution.py:348

commit v7 on v6

--- a/solution.py
+++ b/solution.py
@@ -23,7 +23,7 @@
 def _kernel(nb, q_in, do_in, k_in, v_in, o_in, lse_in, dq_out, dk_out, dv_out,
             raw, lsev, xs, auxs, rx, rs, axr, kt, dk, dv, dqt, dqp, okv, oq, orx,
             raw_l, first_l, lse_l, in_s, in_r, fw_s, fw_r, ax_s, ax_r, fa_s, fa_r, kv_s, kv_r,
-            qp_s, qp_r, oq_s, oq_r):
+            qp_s, qp_r, oq_s, oq_r, ready):
     hd = q_in.shape[-1]
     tile = 4 * ROWS
     scale = hd ** -0.5
@@ -76,7 +76,7 @@
         return remote(oq.at[b, rel[d]], orx.at[b, 0, chip], oq_s.at[0], oq_r.at[g], rel[d] * 2 + core)
 
     barrier = pltpu.get_barrier_semaphore()
-    peers = [r * 2 + core for r in rel] + [sib]
+    peers = [rel[0] * 2 + core, rel[1] * 2 + core, sib]
     for p in peers:
         pl.semaphore_signal(barrier, inc=1, device_id={'cp': p}, device_id_type=MESH)
 
@@ -118,14 +118,23 @@
         raw_copy(i, last_block, first_l.at[i]).wait()
         xs[last_block, :, i] = jnp.swapaxes(raw[last_block, i], 0, 1)
         if i == 0:
-            pl.semaphore_wait(barrier, 4)
-        for d in (2, 0, 1):
+            pl.semaphore_wait(barrier, 3)
+            pl.semaphore_signal(ready, inc=1, device_id={'cp': peers[0]}, device_id_type=MESH)
+        for d in (0, 1):
             in_piece(last_block, d, i).start()
     load(nb - 2)
     load(nb - 3)
-    raw_copy(4, last_block, first_l.at[4]).wait()
+    relayout(nb - 2)
+    for d in (0, 1):
+        in_send(nb - 2, d).start()
+    load(nb - 4)
+    pl.semaphore_wait(ready, 1)
+    in_send(nb - 1, 2).start()
+    in_send(nb - 2, 2).start()
+    raw_copy(4, nb - 1, first_l.at[4]).wait()
     lse_copy.wait()
     stats(nb - 1)
+    stats(nb - 2)
 
     def issue(n, c):
         b = nb - 1 - n
@@ -139,7 +148,7 @@
         stats(b)
         return c
 
-    lax.fori_loop(1, nb, issue, 0)
+    lax.fori_loop(2, nb, issue, 0)
 
     kidx = lax.broadcasted_iota(jnp.int32, (tile, 1), 0)
     qidx = lax.broadcasted_iota(jnp.int32, (1, tile), 1)
@@ -194,10 +203,10 @@
         forward(b).wait_recv()
         aux_forwarded(b).wait_recv()
 
-    def emit_kv(b, g):
+    def emit_kv(b, g, order=(2, 0, 1)):
         okv[b, 0] = (dk[...] * scale).astype(BF16).reshape(4, ROWS, hd)
         okv[b, 1] = dv[...].astype(BF16).reshape(4, ROWS, hd)
-        for d in (2, 0, 1):
+        for d in order:
             kv_send(b, d, g).start()
         orx[b, 1:3, chip] = okv[b, :, chip]
 
@@ -225,11 +234,11 @@
     arrive(nb - 1)
     lax.fori_loop(0, nb - 1, step, 0)
 
-    def finish(i, g):
+    def finish(i, g, order=(2, 0, 1)):
         part_send(i).wait_recv()
         total = (dqt[0, i] + dqp[i]) * scale
         oq[i] = total.T.astype(BF16).reshape(4, ROWS, hd)
-        for d in (2, 0, 1):
+        for d in order:
             q_send(i, d, g).start()
         orx[i, 0, chip] = oq[i, chip]
 
@@ -252,9 +261,13 @@
     pair(0, 0, True, True)
     part_send(0).start()
     pair(0, 0, False, True)
-    emit_kv(0, 2)
-    finish(1, 2)
-    finish(0, 3)
+    emit_kv(0, 2, (2,))
+    finish(1, 2, (2,))
+    finish(0, 3, (2,))
+    for d in (0, 1):
+        kv_send(0, d, 2).start()
+        q_send(1, d, 2).start()
+        q_send(0, d, 3).start()
 
     def put(a, b):
         (dq_out, dk_out, dv_out)[a][rows(b)] = jnp.swapaxes(orx[b, a], 0, 1)
@@ -340,6 +353,7 @@
                 dma((1,)), dma((3,)),
                 dma((1,)), dma((nb,)),
                 dma((1,)), dma((4,)),
+                pltpu.SemaphoreType.REGULAR,
             ],
             compiler_params=pltpu.CompilerParams(
                 collective_id=0, has_side_effects=True, vmem_limit_bytes=VMEM_LIMIT),

time: 87.5 us -> 87.3 us (level)
  no operation moved by 1% of the time
where the time goes in v7:
time: 87.3 us; the launch traced here: 87.1 us
  Pallas kernels  86.4 us (99%)
    pallas_call x1, Pallas kernels, local(): pl.pallas_call(functools.partial(_kernel, nb), out_shape=[jax.ShapeDtypeS...  84.7 us

profile of v7, /device:TPU:0, one launch (start us, length us, event | category | flops | bytes accessed | tf_op | source)
XLA Modules:
  0.0 87.1 jit_solution(11738139701813844628)
XLA Ops:
  0.6 84.7 %attn_bwd.1 = (bf16[1024,4,128]{2,1,0:T(4,128)(2,1)S(1)}, bf16[1024,4,128]{2,1,0:T(4,128)(2,1)S(1)}, bf16[1024,4,128]{2,1,0:T(4,128)(2,1)S(1)}) custom-call(bf16[1024,4,128]{2,1,0:T(4,128)(2,1)} %q_in.1, bf16[1024,4,128]{2,1,0:T(4,128)(2,1)} %do_in.1, bf16[1024,4,128]{2,1,0:T(4,128)(2,1)} %k_in.1, bf16[1024,4,128]{2,1,0:T(4,128)(2,1)} %v_in.1, ...), custom_call_target="tpu_custom_call" | custom-call | tf_op jit(solution)/shard_map/attn_bwd/pallas_call | solution.py:327
  85.4 1.7 %store.1 = (bf16[1024,4,128]{2,1,0:T(4,128)(2,1)}, bf16[1024,4,128]{2,1,0:T(4,128)(2,1)}, bf16[1024,4,128]{2,1,0:T(4,128)(2,1)}) custom-call(bf16[1024,4,128]{2,1,0:T(4,128)(2,1)S(1)} %get-tuple-element.6.a, bf16[1024,4,128]{2,1,0:T(4,128)(2,1)S(1)} %get-tuple-element.7.b, bf16[1024,4,128]{2,1,0:T(4,128)(2,1)S(1)} %get-tuple-element.8.c), custom_call_target="tpu_custom_call" | custom-call | tf_op jit(solution)/shard_map/store/pallas_call | solution.py:362

commit v8 on v7

--- a/solution.py
+++ b/solution.py
@@ -70,11 +70,12 @@
         return remote(okv.at[b, :, rel[d]], orx.at[b, 1:3, chip], kv_s.at[0], kv_r.at[g], rel[d] * 2 + core)
 
     def part_send(b):
-        return remote(dqt.at[1, b], dqp.at[b], qp_s.at[0], qp_r.at[b], sib)
+        return remote(dqt.at[1, b], dqp.at[b], qp_s.at[0], qp_r.at[b % 4], sib)
 
     def q_send(b, d, g):
         return remote(oq.at[b, rel[d]], orx.at[b, 0, chip], oq_s.at[0], oq_r.at[g], rel[d] * 2 + core)
 
+    raw_copy(0, nb - 1, first_l.at[0]).start()
     barrier = pltpu.get_barrier_semaphore()
     peers = [rel[0] * 2 + core, rel[1] * 2 + core, sib]
     for p in peers:
@@ -84,7 +85,7 @@
         for i in range(5):
             raw_copy(i, b, raw_l.at[b % 2]).start()
 
-    for i in range(5):
+    for i in range(1, 5):
         raw_copy(i, nb - 1, first_l.at[i]).start()
     lse_copy = pltpu.make_async_copy(lse_in, lsev, lse_l.at[0])
     lse_copy.start()
@@ -351,7 +352,7 @@
                 dma((1,)), dma((nb,)),
                 dma((1,)), dma((2,)),
                 dma((1,)), dma((3,)),
-                dma((1,)), dma((nb,)),
+                dma((1,)), dma((4,)),
                 dma((1,)), dma((4,)),
                 pltpu.SemaphoreType.REGULAR,
             ],

time: 87.3 us -> 87.2 us (level)
  no operation moved by 1% of the time
where the time goes in v8:
time: 87.2 us; the launch traced here: 86.9 us
  Pallas kernels  86.3 us (99%)
    pallas_call x1, Pallas kernels, local(): pl.pallas_call(functools.partial(_kernel, nb), out_shape=[jax.ShapeDtypeS...  84.6 us

profile of v8, /device:TPU:0, one launch (start us, length us, event | category | flops | bytes accessed | tf_op | source)
XLA Modules:
  0.0 86.9 jit_solution(16498011971961386437)
XLA Ops:
  0.6 84.6 %attn_bwd.1 = (bf16[1024,4,128]{2,1,0:T(4,128)(2,1)S(1)}, bf16[1024,4,128]{2,1,0:T(4,128)(2,1)S(1)}, bf16[1024,4,128]{2,1,0:T(4,128)(2,1)S(1)}) custom-call(bf16[1024,4,128]{2,1,0:T(4,128)(2,1)} %q_in.1, bf16[1024,4,128]{2,1,0:T(4,128)(2,1)} %do_in.1, bf16[1024,4,128]{2,1,0:T(4,128)(2,1)} %k_in.1, bf16[1024,4,128]{2,1,0:T(4,128)(2,1)} %v_in.1, ...), custom_call_target="tpu_custom_call" | custom-call | tf_op jit(solution)/shard_map/attn_bwd/pallas_call | solution.py:328
  85.3 1.7 %store.1 = (bf16[1024,4,128]{2,1,0:T(4,128)(2,1)}, bf16[1024,4,128]{2,1,0:T(4,128)(2,1)}, bf16[1024,4,128]{2,1,0:T(4,128)(2,1)}) custom-call(bf16[1024,4,128]{2,1,0:T(4,128)(2,1)S(1)} %get-tuple-element.6.a, bf16[1024,4,128]{2,1,0:T(4,128)(2,1)S(1)} %get-tuple-element.7.b, bf16[1024,4,128]{2,1,0:T(4,128)(2,1)S(1)} %get-tuple-element.8.c), custom_call_target="tpu_custom_call" | custom-call | tf_op jit(solution)/shard_map/store/pallas_call | solution.py:363
